TPU v7x, 16 devices: a 4x2x1 block of a 4x4x8 slice. The times are simulated.
16 devices in a mesh: replica: 2 (over y, z), model: 8 (over x, core).
Axes of the slice: x: 4, y: 2, z: 1, core: 2. Of those that a mesh axis runs over, the one named last changes fastest.
The devices are a block of a 4x4x8 slice.
Arguments:
- prompt: bfloat16 [64, 384, 3072], P('replica', 'model'), parts along dimension 0
- lengths: int32 [64], P('replica'), parts along dimension 0
- new_tok: bfloat16 [64, 3072], P('replica'), parts along dimension 0
- norm_attn: bfloat16 [1, 3072], replicated
- w_q: bfloat16 [1, 3072, 3072], P(None, None, 'model')
- w_k: bfloat16 [1, 3072, 1024], P(None, None, 'model')
- w_v: bfloat16 [1, 3072, 1024], P(None, None, 'model')
- w_o: bfloat16 [1, 3072, 3072], P(None, 'model')
- norm_mlp: bfloat16 [1, 3072], replicated
- w_gate: bfloat16 [1, 3072, 8192], P(None, None, 'model')
- w_up: bfloat16 [1, 3072, 8192], P(None, None, 'model')
- w_down: bfloat16 [1, 8192, 3072], P(None, 'model')
Outputs:
- output 1: bfloat16 [64, 3072], P('replica'), parts along dimension 0
- output 2: bfloat16 [64, 3072], P('replica'), parts along dimension 0
- output 3: bfloat16 [1, 64, 385, 8, 128], P(None, 'replica', None, 'model'), parts along dimension 1
- output 4: bfloat16 [1, 64, 385, 8, 128], P(None, 'replica', None, 'model'), parts along dimension 1
There are 2 independent parts. A program takes and returns all parts, laid end to end along the dimension named above; an argument that names none is the same for every part.
All inputs are finite; a program needn't handle non-finite values.
Results may differ from a plain program's by a relative error of at most 0.0109076.
Values are sent between devices in bfloat16 or wider.
A program may use at most 768 MiB of HBM per device.

v0:
```python
import jax
import jax.numpy as jnp
from jax import lax
from jax.sharding import PartitionSpec as P

HEAD_DIM = 128
NEG_BIG = -1e30


def rms_norm(hidden, gain_vec):
    hid_f32 = hidden.astype(jnp.float32)
    inv_rms = lax.rsqrt(jnp.mean(hid_f32 * hid_f32, axis=-1, keepdims=True) + 1e-5)
    return (hid_f32 * inv_rms * gain_vec.astype(jnp.float32)).astype(jnp.bfloat16)


def rotary(heads_f32, positions):
    half_dim = HEAD_DIM // 2
    inv_freq = 10000.0 ** (-2.0 * jnp.arange(half_dim, dtype=jnp.float32) / HEAD_DIM)
    angles = positions.astype(jnp.float32)[..., None] * inv_freq
    cos_tab = jnp.cos(angles)[..., None, :]
    sin_tab = jnp.sin(angles)[..., None, :]
    lo_half = heads_f32[..., :half_dim]
    hi_half = heads_f32[..., half_dim:]
    return jnp.concatenate([lo_half * cos_tab - hi_half * sin_tab, hi_half * cos_tab + lo_half * sin_tab], axis=-1)


def block_attention(q_block, key_blocks, val_blocks, lengths, q_start, n_used):
    n_batch, blk_len, n_heads, _ = q_block.shape
    kv_heads = key_blocks.shape[3]
    n_group = n_heads // kv_heads
    q_grouped = q_block.reshape(n_batch, blk_len, kv_heads, n_group, HEAD_DIM)
    q_pos = q_start + jnp.arange(blk_len)
    score_scale = HEAD_DIM ** -0.5

    def step_fn(blk_idx, loop_state):
        run_max, run_sum, run_acc = loop_state
        key_blk = lax.dynamic_index_in_dim(key_blocks, blk_idx, axis=0, keepdims=False)
        val_blk = lax.dynamic_index_in_dim(val_blocks, blk_idx, axis=0, keepdims=False)
        k_pos = blk_idx * blk_len + jnp.arange(blk_len)
        scores = jnp.einsum('bqhgd,bkhd->bqhgk', q_grouped, key_blk, preferred_element_type=jnp.float32) * score_scale
        visible = (k_pos[None, None, :] <= q_pos[None, :, None]) & (k_pos[None, None, :] < lengths[:, None, None])
        scores = jnp.where(visible[:, :, None, None, :], scores, NEG_BIG)
        new_max = jnp.maximum(run_max, jnp.max(scores, axis=-1))
        rescale = jnp.exp(run_max - new_max)
        attn_prob = jnp.exp(scores - new_max[..., None])
        run_sum = run_sum * rescale + jnp.sum(attn_prob, axis=-1)
        run_acc = run_acc * rescale[..., None] + jnp.einsum('bqhgk,bkhd->bqhgd', attn_prob.astype(jnp.bfloat16), val_blk, preferred_element_type=jnp.float32)
        return new_max, run_sum, run_acc

    stat_shape = (n_batch, blk_len, kv_heads, n_group)
    init_state = (jnp.full(stat_shape, NEG_BIG, jnp.float32), jnp.zeros(stat_shape, jnp.float32), jnp.zeros(stat_shape + (HEAD_DIM,), jnp.float32))
    run_max, run_sum, run_acc = lax.fori_loop(0, n_used, step_fn, init_state)
    return (run_acc / run_sum[..., None]).reshape(n_batch, blk_len, n_heads * HEAD_DIM).astype(jnp.bfloat16)


def decode_attention(q_new, key_cache, val_cache, lengths):
    n_batch, n_heads, _ = q_new.shape
    kv_heads = key_cache.shape[2]
    cache_len = key_cache.shape[1]
    q_grouped = q_new.reshape(n_batch, kv_heads, n_heads // kv_heads, HEAD_DIM)
    scores = jnp.einsum('bhgd,bkhd->bhgk', q_grouped, key_cache, preferred_element_type=jnp.float32) * (HEAD_DIM ** -0.5)
    cache_pos = jnp.arange(cache_len)
    visible = (cache_pos[None, :] < lengths[:, None]) | (cache_pos[None, :] == cache_len - 1)
    scores = jnp.where(visible[:, None, None, :], scores, NEG_BIG)
    attn_prob = jax.nn.softmax(scores, axis=-1)
    out_f32 = jnp.einsum('bhgk,bkhd->bhgd', attn_prob.astype(jnp.bfloat16), val_cache, preferred_element_type=jnp.float32)
    return out_f32.reshape(n_batch, n_heads * HEAD_DIM).astype(jnp.bfloat16)


def decode_layer(dec_hidden, key_mine, val_mine, lengths, gain_attn, wq_loc, wk_loc, wv_loc, wo_loc, gain_mlp, wg_loc, wu_loc, wd_loc):
    n_batch = dec_hidden.shape[0]
    heads_loc = wq_loc.shape[1] // HEAD_DIM
    kv_loc = wk_loc.shape[1] // HEAD_DIM
    tok_norm = rms_norm(dec_hidden, gain_attn)
    q_new = rotary(jnp.dot(tok_norm, wq_loc, preferred_element_type=jnp.float32).reshape(n_batch, heads_loc, HEAD_DIM), lengths).astype(jnp.bfloat16)
    k_new = rotary(jnp.dot(tok_norm, wk_loc, preferred_element_type=jnp.float32).reshape(n_batch, kv_loc, HEAD_DIM), lengths).astype(jnp.bfloat16)
    v_new = jnp.dot(tok_norm, wv_loc, preferred_element_type=jnp.float32).astype(jnp.bfloat16).reshape(n_batch, kv_loc, HEAD_DIM)
    key_cache = jnp.concatenate([key_mine, k_new[:, None]], axis=1)
    val_cache = jnp.concatenate([val_mine, v_new[:, None]], axis=1)
    tok_attn = decode_attention(q_new, key_cache, val_cache, lengths)
    attn_part = jnp.dot(tok_attn, wo_loc, preferred_element_type=jnp.float32)
    dec_hidden = (dec_hidden.astype(jnp.float32) + lax.psum(attn_part, 'model')).astype(jnp.bfloat16)
    tok_norm = rms_norm(dec_hidden, gain_mlp)
    tok_mid = (jax.nn.silu(jnp.dot(tok_norm, wg_loc, preferred_element_type=jnp.float32)) * jnp.dot(tok_norm, wu_loc, preferred_element_type=jnp.float32)).astype(jnp.bfloat16)
    mlp_part = jnp.dot(tok_mid, wd_loc, preferred_element_type=jnp.float32)
    dec_hidden = (dec_hidden.astype(jnp.float32) + lax.psum(mlp_part, 'model')).astype(jnp.bfloat16)
    return dec_hidden, key_cache, val_cache


def solution(mesh):
    n_dev = mesh.shape['model']
    seq_spec = P('replica', 'model', None)
    col_spec = P(None, None, 'model')
    row_spec = P(None, 'model', None)
    gain_spec = P(None, None)
    tok_spec = P('replica', None)
    cache_spec = P(None, 'replica', None, 'model', None)
    in_specs = (seq_spec, P('replica'), tok_spec, gain_spec, col_spec, col_spec, col_spec, row_spec, gain_spec, col_spec, col_spec, row_spec)
    out_specs = (tok_spec, tok_spec, cache_spec, cache_spec)

    def per_device(prompt, lengths, new_tok, norm_attn, w_q, w_k, w_v, w_o, norm_mlp, w_gate, w_up, w_down):
        my_idx = lax.axis_index('model')
        n_batch, seq_loc, d_model = prompt.shape
        n_tok = n_batch * seq_loc
        kv_loc = w_k.shape[2] // HEAD_DIM
        n_heads = (w_q.shape[2] // HEAD_DIM) * n_dev
        kv_heads = kv_loc * n_dev
        seq_len = seq_loc * n_dev
        seq_pos = my_idx * seq_loc + jnp.arange(seq_loc)
        hidden = prompt
        dec_hidden = new_tok
        key_layers = []
        val_layers = []
        for layer_idx in range(w_q.shape[0]):
            wq_full = lax.all_gather(w_q[layer_idx], 'model', axis=1, tiled=True)
            wk_full = lax.all_gather(w_k[layer_idx], 'model', axis=1, tiled=True)
            wv_full = lax.all_gather(w_v[layer_idx], 'model', axis=1, tiled=True)
            wo_full = lax.all_gather(w_o[layer_idx], 'model', axis=0, tiled=True)
            wg_full = lax.all_gather(w_gate[layer_idx], 'model', axis=1, tiled=True)
            wu_full = lax.all_gather(w_up[layer_idx], 'model', axis=1, tiled=True)
            wd_full = lax.all_gather(w_down[layer_idx], 'model', axis=0, tiled=True)
            normed = rms_norm(hidden, norm_attn[layer_idx]).reshape(n_tok, d_model)
            q_rot = rotary(jnp.dot(normed, wq_full, preferred_element_type=jnp.float32).reshape(n_batch, seq_loc, n_heads, HEAD_DIM), seq_pos).astype(jnp.bfloat16)
            k_rot = rotary(jnp.dot(normed, wk_full, preferred_element_type=jnp.float32).reshape(n_batch, seq_loc, kv_heads, HEAD_DIM), seq_pos).astype(jnp.bfloat16)
            v_proj = jnp.dot(normed, wv_full, preferred_element_type=jnp.float32).astype(jnp.bfloat16).reshape(n_batch, seq_loc, kv_heads, HEAD_DIM)
            key_blocks = lax.all_gather(k_rot, 'model', axis=0)
            val_blocks = lax.all_gather(v_proj, 'model', axis=0)
            attn_out = block_attention(q_rot, key_blocks, val_blocks, lengths, my_idx * seq_loc, my_idx + 1).reshape(n_tok, n_heads * HEAD_DIM)
            hidden = (hidden.astype(jnp.float32) + jnp.dot(attn_out, wo_full, preferred_element_type=jnp.float32).reshape(n_batch, seq_loc, d_model)).astype(jnp.bfloat16)
            normed = rms_norm(hidden, norm_mlp[layer_idx]).reshape(n_tok, d_model)
            mlp_mid = (jax.nn.silu(jnp.dot(normed, wg_full, preferred_element_type=jnp.float32)) * jnp.dot(normed, wu_full, preferred_element_type=jnp.float32)).astype(jnp.bfloat16)
            hidden = (hidden.astype(jnp.float32) + jnp.dot(mlp_mid, wd_full, preferred_element_type=jnp.float32).reshape(n_batch, seq_loc, d_model)).astype(jnp.bfloat16)
            key_mine = jnp.moveaxis(lax.dynamic_slice_in_dim(key_blocks, my_idx * kv_loc, kv_loc, axis=3), 0, 1).reshape(n_batch, seq_len, kv_loc, HEAD_DIM)
            val_mine = jnp.moveaxis(lax.dynamic_slice_in_dim(val_blocks, my_idx * kv_loc, kv_loc, axis=3), 0, 1).reshape(n_batch, seq_len, kv_loc, HEAD_DIM)
            dec_hidden, key_cache, val_cache = decode_layer(dec_hidden, key_mine, val_mine, lengths, norm_attn[layer_idx], w_q[layer_idx], w_k[layer_idx], w_v[layer_idx], w_o[layer_idx], norm_mlp[layer_idx], w_gate[layer_idx], w_up[layer_idx], w_down[layer_idx])
            key_layers.append(key_cache)
            val_layers.append(val_cache)
        last_sel = (seq_pos[None, :] == (lengths - 1)[:, None]).astype(jnp.bfloat16)
        last_part = jnp.einsum('bs,bsd->bd', last_sel, hidden, preferred_element_type=jnp.float32)
        last_hidden = lax.psum(last_part, 'model').astype(jnp.bfloat16)
        return dec_hidden, last_hidden, jnp.stack(key_layers), jnp.stack(val_layers)

    return jax.shard_map(per_device, mesh=mesh, in_specs=in_specs, out_specs=out_specs, check_vma=False)
```

profile of v0, /device:TPU:112, one launch (start us, length us, event | category | flops | bytes accessed | tf_op | source)
XLA Modules:
  0.0 1509.9 jit_solution(9331472075091081530)
XLA Ops:
  7.2 0.7 all-gather.23.cloned.1.call-update
  8.0 0.7 all-gather.21.cloned.1.call-update
  8.9 0.7 mul.360
  9.6 5.6 fusion.25
  15.2 11.2 fusion.27
  26.4 25.8 %all-gather.23.cloned.1.call-done = bf16[1,3072,1024]{2,1,0:T(8,128)(2,1)} async-done(((bf16[1,3072,128]{2,1,0:T(8,128)(2,1)}), bf16[1,3072,1024]{2,1,0:T(8,128)(2,1)}) %all-gather.23.cloned.1.call-update) | async-done | bytes 6291472 | tf_op jit(solution)/shard_map/all_gather | solution.py:117
  52.2 14.0 fusion.64
  66.2 2.5 copy.64
  69.2 25.1 %all-gather.21.cloned.1.call-done = bf16[1,3072,1024]{2,1,0:T(8,128)(2,1)} async-done(((bf16[1,3072,128]{2,1,0:T(8,128)(2,1)}), bf16[1,3072,1024]{2,1,0:T(8,128)(2,1)}) %all-gather.21.cloned.1.call-update) | async-done | bytes 6291472 | tf_op jit(solution)/shard_map/all_gather | solution.py:116
  94.3 8.6 copy.42
  102.9 13.0 fusion.39
  116.0 2.3 fusion.58
  118.4 1.7 pad_maximum_fusion.3
  120.1 2.5 copy.43
  123.4 1.4 convolution_bitcast_fusion
  125.2 2.6 copy.41
  127.9 2.5 fusion.97
  130.7 83.5 %all-gather.19.cloned.1.call-done = bf16[8,32,48,8,128]{4,3,2,1,0:T(8,128)(2,1)} async-done(((bf16[1,32,48,8,128]{4,3,2,1,0:T(8,128)(2,1)}), bf16[8,32,48,8,128]{4,3,2,1,0:T(8,128)(2,1)}) %all-gather.19.cloned.1.call-update) | async-done | bytes 25165840 | tf_op jit(solution)/shard_map/all_gather | solution.py:127
  214.1 119.6 %all-gather.17.cloned.1.call-done = bf16[8,32,48,8,128]{4,3,2,1,0:T(8,128)(2,1)} async-done(((bf16[1,32,48,8,128]{4,3,2,1,0:T(8,128)(2,1)}), bf16[8,32,48,8,128]{4,3,2,1,0:T(8,128)(2,1)}) %all-gather.17.cloned.1.call-update) | async-done | bytes 25165840 | tf_op jit(solution)/shard_map/all_gather | solution.py:126
  333.8 26.6 %dynamic-slice_bitcast_fusion = (bf16[32,8,48,1,128]{4,3,2,0,1:T(2,128)(2,1)}, bf16[8,32,48,1,128]{4,3,2,1,0:T(2,128)(2,1)}) fusion(bf16[8,32,48,8,128]{4,3,2,1,0:T(8,128)(2,1)} %all-gather.19.cloned.1.call-done, s32[]{:T(128)S(6)} %select_n.18, bf16[8,32,48,8,128]{4,3,2,1,0:T(8,128)(2,1)} %all-gather.17.cloned.1.call-done), kind=kLoop, calls=%fused_computation.67 | loop fusion | bytes 12582916 | tf_op jit(solution)/shard_map/transpose | solution.py:134
  360.4 3.7 copy.47
  364.1 0.9 copy-done.3
  365.0 2.5 copy.63
  367.4 3.9 fusion.132
  371.4 1.7 fusion.78
  373.1 2.9 fusion.60
  376.8 0.7 all-gather.27.cloned.1.call-update
  377.6 52.1 %all-reduce.4.cloned.1.call-done = f32[32,3072]{1,0:T(8,128)} async-done(((f32[32,3072]{1,0:T(8,128)}), f32[32,3072]{1,0:T(8,128)}) %all-reduce.4.cloned.1.call-update) | async-done | bytes 393232 | tf_op jit(solution)/shard_map/psum | solution.py:82
  429.7 1.2 fusion.93
  430.9 4.1 fusion.47
  435.0 7.7 fusion.43
  442.8 0.7 all-gather.29.cloned.1.call-update
  445.0 0.7 compare_bitcast_fusion
  445.7 74.2 %all-gather.25.cloned.1.call-done = bf16[1,3072,3072]{2,1,0:T(8,128)(2,1)} async-done(((bf16[1,3072,384]{2,1,0:T(8,128)(2,1)}), bf16[1,3072,3072]{2,1,0:T(8,128)(2,1)}) %all-gather.25.cloned.1.call-update) | async-done | bytes 18874384 | tf_op jit(solution)/shard_map/all_gather | solution.py:115
  519.9 24.6 %copy.49 = bf16[3072,3072]{1,0:T(8,128)(2,1)} copy(bf16[3072,3072]{0,1:T(8,128)(2,1)} %bitcast.185) | data formatting | bytes 37748736 | tf_op jit(solution)/shard_map/dot_general | solution.py:123
  544.5 36.9 %fusion.37 = f32[32,48,24,128]{3,1,2,0:T(8,128)} fusion(bf16[24,128,3072,1]{2,1,0,3:T(8,128)(2,1)} %bitcast.187, bf16[32,48,3072]{2,1,0:T(8,128)(2,1)} %fusion.27), kind=kOutput, calls=%fused_computation.55 | convolution fusion | flops 28991029248 | bytes 47185920 | tf_op jit(solution)/shard_map/dot_general | solution.py:123
  581.4 13.9 subtract_convert_fusion
  595.3 6.7 pad_maximum_fusion
  602.0 0.9 broadcast_in_dim.35
  602.9 0.9 broadcast_in_dim.36
  603.9 8.5 broadcast_in_dim.37
  612.4 59.4 %while.15 = (s32[]{:T(128)}, f32[32,48,8,3]{1,3,2,0:T(4,128)}, f32[32,48,8,3]{1,3,2,0:T(4,128)}, f32[32,48,8,3,128]{4,1,3,2,0:T(8,128)}, s32[]{:T(128)}, /*index...) while((s32[]{:T(128)}, f32[32,48,8,3]{1,3,2,0:T(4,128)}, ...), condition=%wide.region_10.11_spmd.clone, body=%wide.region_7.10_spmd.clone.sunk | while | flops 935022464 | bytes 91726680 | solution.py:52
  613.0 5.1 constant_dynamic-slice_fusion.4
  618.1 20.6 %fusion.152 = (f32[32,48,8,3]{1,3,2,0:T(4,128)}, f32[32,8,48,48,3]{3,2,4,1,0:T(8,128)}) fusion(pred[32,48,48]{1,2,0:T(8,128)(4,1)S(1)} %broadcast_and_fusion.2, bf16[32,48,8,3,128]{4,1,3,2,0:T(8,128)(2,1)} %get-tuple-element.269, bf16[1,32,48,8,128]{4,3,2,1,0:T(8,128)(2,1)} %get-tuple-element.228), kind=kOutput, calls=%fused_computation.6.clone.1 | convolution fusion | flops 458256384 | bytes 19881984 | tf_op jit(solution)/shard_map/while/body/bqhgd,bkhd->bqhgk/dot_general | solution.py:40
  638.7 1.4 max.7
  640.1 9.6 fusion.153
  650.2 0.8 copy.99
  651.0 20.6 %bitcast_add_fusion.2 = f32[32,48,8,3,128]{4,1,3,2,0:T(8,128)} fusion(f32[32,48,8,3,128]{4,1,3,2,0:T(8,128)} %get-tuple-element.251, f32[32,48,8,3]{1,3,2,0:T(4,128)S(1)} %get-tuple-element.232, f32[32,8,48,48,3]{3,2,4,1,0:T(8,128)} %get-tuple-element.230, f32[32,48,8,3]{1,3,2,0:T(4,128)S(1)} %max.7, ...), kind=kOutput, calls=%fused_computation.1.clone.1 | convolution fusion | flops 469499904 | bytes 48340992 | tf_op jit(solution)/shard_map/while/body/bqhgk,bkhd->bqhgd/dot_general | solution.py:47
  671.8 10.7 divide_convert_fusion
  682.5 11.5 copy.52
  694.0 23.7 %convert_element_type.145 = bf16[32,48,3072]{2,1,0:T(8,128)(2,1)} reshape(bf16[32,48,8,3,128]{4,3,2,1,0:T(4,128)(2,1)} %copy.52) | data formatting | bytes 18874368 | tf_op jit(solution)/shard_map/convert_element_type | solution.py:53
  718.0 2.1 copy.53
  720.4 2.1 copy.54
  722.5 38.4 %fusion.29 = (f32[32,48]{1,0:T(8,128)S(1)}, bf16[32,48,3072]{2,1,0:T(8,128)(2,1)}) fusion(bf16[32,48,3072]{2,1,0:T(8,128)(2,1)} %convert_element_type.145, bf16[1,3072,3072]{2,1,0:T(8,128)(2,1)} %all-gather.27.cloned.1.call-done, bf16[32,48,3072]{2,1,0:T(8,128)(2,1)} %param.14), kind=kOutput, calls=%fused_computation.44 | convolution fusion | flops 29019338752 | bytes 47192064 | tf_op jit(solution)/shard_map/dot_general | solution.py:129
  761.0 11.3 fusion.31
  772.3 1.7 fusion.96
  774.0 118.3 %all-gather.29.cloned.1.call-done = bf16[1,3072,8192]{2,1,0:T(8,128)(2,1)} async-done(((bf16[1,3072,1024]{2,1,0:T(8,128)(2,1)}), bf16[1,3072,8192]{2,1,0:T(8,128)(2,1)}) %all-gather.29.cloned.1.call-update) | async-done | bytes 50331664 | tf_op jit(solution)/shard_map/all_gather | solution.py:119
  892.3 88.4 %fusion.21 = f32[1536,8192]{1,0:T(8,128)} fusion(bf16[1536,3072]{1,0:T(8,128)(2,1)} %bitcast.195, bf16[1,3072,8192]{2,1,0:T(8,128)(2,1)} %all-gather.29.cloned.1.call-done), kind=kOutput, calls=%fused_computation.31 | convolution fusion | flops 77309411328 | bytes 110100480 | tf_op jit(solution)/shard_map/dot_general | solution.py:131
  980.7 136.6 %all-gather.31.cloned.1.call-done = bf16[1,3072,8192]{2,1,0:T(8,128)(2,1)} async-done(((bf16[1,3072,1024]{2,1,0:T(8,128)(2,1)}), bf16[1,3072,8192]{2,1,0:T(8,128)(2,1)}) %all-gather.31.cloned.1.call-update) | async-done | bytes 50331664 | tf_op jit(solution)/shard_map/all_gather | solution.py:120
  1117.3 95.1 %multiply_convert_fusion = bf16[1536,8192]{1,0:T(8,128)(2,1)} fusion(f32[1536,8192]{1,0:T(8,128)} %fusion.21, bf16[1536,3072]{1,0:T(8,128)(2,1)} %bitcast.196, bf16[1,3072,8192]{2,1,0:T(8,128)(2,1)} %all-gather.31.cloned.1.call-done), kind=kOutput, calls=%fused_computation.33 | convolution fusion | flops 77384908800 | bytes 135266304 | tf_op jit(solution)/shard_map/dot_general | solution.py:131
  1212.4 130.1 %all-gather.33.cloned.1.call-done = bf16[1,8192,3072]{2,1,0:T(8,128)(2,1)} async-done(((bf16[1,1024,3072]{2,1,0:T(8,128)(2,1)}), bf16[1,8192,3072]{2,1,0:T(8,128)(2,1)}) %all-gather.33.cloned.1.call-update) | async-done | bytes 50331664 | tf_op jit(solution)/shard_map/all_gather | solution.py:121
  1342.5 92.1 %fusion.17 = f32[1536,3072]{1,0:T(8,128)} fusion(bf16[1536,8192]{1,0:T(8,128)(2,1)} %multiply_convert_fusion, bf16[1,8192,3072]{2,1,0:T(8,128)(2,1)} %all-gather.33.cloned.1.call-done), kind=kOutput, calls=%fused_computation.27 | convolution fusion | flops 77309411328 | bytes 94371840 | tf_op jit(solution)/shard_map/dot_general | solution.py:132
  1434.6 10.7 fusion.35
  1445.4 57.8 %all-reduce.7 = bf16[32,3072]{1,0:T(8,128)(2,1)} all-reduce(f32[32,3072]{1,0:T(8,128)S(1)} %bitcast.199), channel_id=1, replica_groups=mesh['replica'=2,'model'=8] {'model'}, use_global_device_ids=true, to_apply=%region_12.13 | all-reduce | flops 98304 | bytes 589824 | tf_op jit(solution)/shard_map/psum | solution.py:140
  (90 shorter events, 6.1 us)
Async XLA Ops:
  7.2 45.0 %all-gather.23.cloned.1.call-start = ((), (), s32[]{:S(2)}) async-start(), calls=%async_computation.5 | async-start | bytes 7077888 | tf_op jit(solution)/shard_map/all_gather | solution.py:117
  8.0 86.4 %all-gather.21.cloned.1.call-start = ((), (), s32[]{:S(2)}) async-start(), calls=%async_computation.4 | async-start | bytes 7077888 | tf_op jit(solution)/shard_map/all_gather | solution.py:116
  8.8 205.4 %all-gather.19.cloned.1.call-start = ((), (), s32[]{:S(2)}) async-start(), calls=%async_computation.1 | async-start | bytes 28311552 | tf_op jit(solution)/shard_map/all_gather | solution.py:127
  68.7 265.1 %all-gather.17.cloned.1.call-start = ((), (), s32[]{:S(2)}) async-start(), calls=%async_computation | async-start | bytes 28311552 | tf_op jit(solution)/shard_map/all_gather | solution.py:126
  118.3 4.6 copy-start.8
  118.3 4.8 copy-start.9
  118.3 6.5 copy-start.19
  118.3 6.8 copy-start.7
  122.6 307.1 %all-reduce.4.cloned.1.call-start = ((), (), s32[]{:S(2)}) async-start(), calls=%async_computation.2 | async-start | bytes 786432 | tf_op jit(solution)/shard_map/psum | solution.py:82
  123.4 248.0 %copy-start.15 = (bf16[32,1,1,128]{3,1,0,2:T(2,128)(2,1)}, bf16[32,1,1,128]{3,1,0,2:T(2,128)(2,1)S(1)}, u32[]{:S(2)}) copy-start(bf16[32,1,1,128]{3,1,0,2:T(2,128)(2,1)S(1)} %copy.48) | copy-start | bytes 24580
  125.1 242.3 %copy-start.17 = (bf16[32,1,1,128]{3,1,0,2:T(2,128)(2,1)}, bf16[32,1,1,128]{3,1,0,2:T(2,128)(2,1)S(1)}, u32[]{:S(2)}) copy-start(bf16[32,1,1,128]{3,1,0,2:T(2,128)(2,1)S(1)} %copy.45) | copy-start | bytes 24580
  360.4 4.6 copy-start.3
  364.1 9.0 copy-start.4
  367.4 10.2 copy-start.20
  376.1 143.8 %all-gather.25.cloned.1.call-start = ((), (), s32[]{:S(2)}) async-start(), calls=%async_computation.6 | async-start | bytes 21233664 | tf_op jit(solution)/shard_map/all_gather | solution.py:115
  376.7 345.8 %all-gather.27.cloned.1.call-start = ((), (), s32[]{:S(2)}) async-start(), calls=%async_computation.7 | async-start | bytes 21233664 | tf_op jit(solution)/shard_map/all_gather | solution.py:118
  377.5 394.8 %all-reduce.6.cloned.1.call-start = ((), (), s32[]{:S(2)}) async-start(), calls=%async_computation.3 | async-start | bytes 786432 | tf_op jit(solution)/shard_map/psum | solution.py:86
  377.6 65.1 %copy-start.12 = (f32[1,3072]{1,0:T(1,128)}, f32[1,3072]{1,0:T(1,128)S(1)}, u32[]{:S(2)}) copy-start(f32[1,3072]{1,0:T(1,128)S(1)} %mul.361) | copy-start | bytes 36868
  430.9 11.8 copy-start.10
  442.8 449.6 %all-gather.29.cloned.1.call-start = ((), (), s32[]{:S(2)}) async-start(), calls=%async_computation.8 | async-start | bytes 56623104 | tf_op jit(solution)/shard_map/all_gather | solution.py:119
  443.6 673.8 %all-gather.31.cloned.1.call-start = ((), (), s32[]{:S(2)}) async-start(), calls=%async_computation.9 | async-start | bytes 56623104 | tf_op jit(solution)/shard_map/all_gather | solution.py:120
  444.2 898.3 %all-gather.33.cloned.1.call-start = ((), (), s32[]{:S(2)}) async-start(), calls=%async_computation.10 | async-start | bytes 56623104 | tf_op jit(solution)/shard_map/all_gather | solution.py:121
  640.1 9.6 copy-start
  640.1 9.6 copy-start.1
  650.2 21.4 %copy-start.2 = (f32[32,48,8,3]{1,3,2,0:T(4,128)}, f32[32,48,8,3]{1,3,2,0:T(4,128)S(1)}, u32[]{:S(2)}) copy-start(f32[32,48,8,3]{1,3,2,0:T(4,128)S(1)} %get-tuple-element.264) | copy-start | bytes 442372 | tf_op jit(solution)/shard_map/while
  694.0 23.7 %copy-start.6 = (bf16[8,32,48,1,128]{4,2,0,1,3:T(8,128)(2,1)S(1)}, bf16[8,32,48,1,128]{4,2,0,1,3:T(8,128)(2,1)}, u32[]{:S(2)}) copy-start(bf16[8,32,48,1,128]{4,2,0,1,3:T(8,128)(2,1)} %copy.63) | copy-start | bytes 9437188
  694.0 23.7 %copy-start.18 = (bf16[32,1,1,128]{3,1,0,2:T(2,128)(2,1)S(1)}, bf16[32,1,1,128]{3,1,0,2:T(2,128)(2,1)}, u32[]{:S(2)}) copy-start(bf16[32,1,1,128]{3,1,0,2:T(2,128)(2,1)} %copy-done.17) | copy-start | bytes 24580
  717.7 2.4 copy-start.5
  717.7 2.4 copy-start.16
  722.5 38.5 %copy-start.13 = (f32[1,3072]{1,0:T(1,128)S(1)}, f32[1,3072]{1,0:T(1,128)}, u32[]{:S(2)}) copy-start(f32[1,3072]{1,0:T(1,128)} %copy-done.12) | copy-start | bytes 36868
  761.0 11.4 copy-start.11
  1212.4 222.1 %copy-start.14 = (pred[32,48,1]{1,0,2:T(32,128)(4,1)S(1)}, pred[32,48,1]{1,0,2:T(32,128)(4,1)}, u32[]{:S(2)}) copy-start(pred[32,48,1]{1,0,2:T(32,128)(4,1)} %compare_bitcast_fusion) | copy-start | bytes 4612
Sparse Core Ops, SparseCore 0:
  9.6 42.5 all-gather.22
  53.7 40.5 all-gather.20
  96.5 117.6 all-gather.18
  216.1 117.5 all-gather.16
  376.2 53.4 all-reduce.3
  431.1 88.6 all-gather.24
  521.4 90.7 all-gather.26
  614.6 53.1 all-reduce.5
  669.4 222.8 all-gather.28
  893.8 223.5 all-gather.30
  1118.9 223.5 all-gather.32
where the time goes:
time: 1520 us; the launch traced here: 1510 us
  waiting for transfers between devices  770 us (51%)
  matrix products  454 us (30%)
  local copies, waits for them, and re-layouts  130 us (9%)
  other arithmetic  81.1 us (5%)
  blocking collectives  57.8 us (4%)
    all_gather x1, waiting for transfers between devices, per_device(): wu_full = lax.all_gather(w_up[layer_idx], 'model', axis=1, tiled=True)  137 us
    all_gather x1, waiting for transfers between devices, per_device(): wd_full = lax.all_gather(w_down[layer_idx], 'model', axis=0, tiled=True)  130 us
    all_gather x1, waiting for transfers between devices, per_device(): key_blocks = lax.all_gather(k_rot, 'model', axis=0)  120 us
    all_gather x1, waiting for transfers between devices, per_device(): wg_full = lax.all_gather(w_gate[layer_idx], 'model', axis=1, tiled=True)  118 us
    dot_general x1, matrix products, per_device(): jnp.dot(normed, wu_full, preferred_element_type=jnp.float32)  95.1 us
    dot_general x1, matrix products, per_device(): jnp.dot(mlp_mid, wd_full, preferred_element_type=jnp.float32)  92.1 us
    dot_general x1, matrix products, per_device(): jnp.dot(normed, wg_full, preferred_element_type=jnp.float32)  88.4 us
    all_gather x1, waiting for transfers between devices, per_device(): val_blocks = lax.all_gather(v_proj, 'model', axis=0)  83.5 us
  transfers between devices with their start and end apart: 11, of which 9 were waited for; matrix products, arithmetic and copies ran while one was open for 34% of the time, Pallas kernels for 0%

commit v1 on v0

v1 whole, which is shorter than its diff:
```python
import jax
import jax.numpy as jnp
from jax import lax
from jax.sharding import PartitionSpec as P

HEAD_DIM = 128
NEG_BIG = -1e30


def rms_norm(hidden, gain_vec):
    hid_f32 = hidden.astype(jnp.float32)
    inv_rms = lax.rsqrt(jnp.mean(hid_f32 * hid_f32, axis=-1, keepdims=True) + 1e-5)
    return (hid_f32 * inv_rms * gain_vec.astype(jnp.float32)).astype(jnp.bfloat16)


def rotary(heads_f32, positions):
    half_dim = HEAD_DIM // 2
    inv_freq = 10000.0 ** (-2.0 * jnp.arange(half_dim, dtype=jnp.float32) / HEAD_DIM)
    angles = positions.astype(jnp.float32)[..., None] * inv_freq
    cos_tab = jnp.cos(angles)[..., None, :]
    sin_tab = jnp.sin(angles)[..., None, :]
    lo_half = heads_f32[..., :half_dim]
    hi_half = heads_f32[..., half_dim:]
    return jnp.concatenate([lo_half * cos_tab - hi_half * sin_tab, hi_half * cos_tab + lo_half * sin_tab], axis=-1)


def dot_f32(a, b):
    return jnp.dot(a, b, preferred_element_type=jnp.float32)


def solution(mesh):
    n_dev = mesh.shape['model']
    seq_spec = P('replica', 'model', None)
    col_spec = P(None, None, 'model')
    row_spec = P(None, 'model', None)
    gain_spec = P(None, None)
    tok_spec = P('replica', None)
    cache_spec = P(None, 'replica', None, 'model', None)
    in_specs = (seq_spec, P('replica'), tok_spec, gain_spec, col_spec, col_spec, col_spec, row_spec, gain_spec, col_spec, col_spec, row_spec)
    out_specs = (tok_spec, tok_spec, cache_spec, cache_spec)

    def per_device(prompt, lengths, new_tok, norm_attn, w_q, w_k, w_v, w_o, norm_mlp, w_gate, w_up, w_down):
        assert w_q.shape[0] == 1
        my_idx = lax.axis_index('model')
        n_batch, seq_loc, d_model = prompt.shape
        n_tok = n_batch * seq_loc
        seq_len = seq_loc * n_dev
        heads_loc = w_q.shape[2] // HEAD_DIM
        g_attn, wq, wk, wv, wo, g_mlp, wg, wu, wd = (a[0] for a in (norm_attn, w_q, w_k, w_v, w_o, norm_mlp, w_gate, w_up, w_down))
        seq_pos = my_idx * seq_loc + jnp.arange(seq_loc)
        wk_full = lax.all_gather(wk, 'model', axis=0, tiled=False)
        wv_full = lax.all_gather(wv, 'model', axis=0, tiled=False)
        normed = rms_norm(prompt, g_attn)
        k_all = jnp.einsum('bsd,jdh->jsbh', normed, wk_full, preferred_element_type=jnp.float32)
        v_all = jnp.einsum('bsd,jdh->jsbh', normed, wv_full, preferred_element_type=jnp.float32).astype(jnp.bfloat16)
        k_all = rotary(k_all, seq_pos).astype(jnp.bfloat16)
        key_mine = lax.all_to_all(k_all, 'model', 0, 0, tiled=False).reshape(seq_len, n_batch, HEAD_DIM)
        val_mine = lax.all_to_all(v_all, 'model', 0, 0, tiled=False).reshape(seq_len, n_batch, HEAD_DIM)
        last_sel = (seq_pos[None, :] == (lengths - 1)[:, None]).astype(jnp.bfloat16)
        last_row = jnp.einsum('bs,bsd->bd', last_sel, prompt, preferred_element_type=jnp.float32)
        last_row = lax.psum(last_row, 'model').astype(jnp.bfloat16)
        rows = jnp.concatenate([last_row, new_tok], axis=0)
        row_pos = jnp.concatenate([lengths - 1, lengths])
        row_norm = rms_norm(rows, g_attn)
        q_rows = rotary(dot_f32(row_norm, wq).reshape(2 * n_batch, heads_loc, HEAD_DIM), row_pos).astype(jnp.bfloat16)
        new_norm = row_norm[n_batch:]
        k_new = rotary(dot_f32(new_norm, wk)[:, None], lengths).astype(jnp.bfloat16)[:, 0]
        v_new = dot_f32(new_norm, wv).astype(jnp.bfloat16)
        key_cache = jnp.concatenate([key_mine, k_new[None]], axis=0)
        val_cache = jnp.concatenate([val_mine, v_new[None]], axis=0)
        q_grp = q_rows.reshape(2, n_batch, heads_loc, HEAD_DIM)
        scores = jnp.einsum('tbgd,kbd->btgk', q_grp, key_cache, preferred_element_type=jnp.float32) * (HEAD_DIM ** -0.5)
        slot = jnp.arange(seq_len + 1)
        old = slot[None, :] < lengths[:, None]
        visible = jnp.stack([old, old | (slot[None, :] == seq_len)], axis=1)
        scores = jnp.where(visible[:, :, None, :], scores, NEG_BIG)
        prob = jax.nn.softmax(scores, axis=-1).astype(jnp.bfloat16)
        attn = jnp.einsum('btgk,kbd->tbgd', prob, val_cache, preferred_element_type=jnp.float32)
        attn = attn.reshape(2 * n_batch, heads_loc * HEAD_DIM).astype(jnp.bfloat16)
        hidden = (rows.astype(jnp.float32) + lax.psum(dot_f32(attn, wo), 'model')).astype(jnp.bfloat16)
        mlp_in = rms_norm(hidden, g_mlp)
        mid = (jax.nn.silu(dot_f32(mlp_in, wg)) * dot_f32(mlp_in, wu)).astype(jnp.bfloat16)
        hidden = (hidden.astype(jnp.float32) + lax.psum(dot_f32(mid, wd), 'model')).astype(jnp.bfloat16)

        def as_cache(arr):
            return jnp.transpose(arr[None, :, :, None, :], (0, 2, 1, 3, 4))

        return hidden[n_batch:], hidden[:n_batch], as_cache(key_cache), as_cache(val_cache)

    return jax.shard_map(per_device, mesh=mesh, in_specs=in_specs, out_specs=out_specs, check_vma=False)
```

time: 1520 us -> 304 us (0.20)
  waiting for transfers between devices: 770 us -> 139 us
  matrix products: 454 us -> 54.8 us
  local copies, waits for them, and re-layouts: 130 us -> 24.8 us
  other arithmetic: 81.1 us -> 21.9 us
  blocking collectives: 57.8 us -> 38.6 us
    all_gather x9 -> x2, waiting for transfers between devices: 713 us -> 3.93 us  [the longest x1 3.91 us: per_device(): wv_full = lax.all_gather(wv, 'model', axis=0, tiled=False)]
    dot_general x17 -> x10, matrix products: 450 us -> 50.7 us  [the longest x6 16.3 us: dot_f32(): return jnp.dot(a, b, preferred_element_type=jnp.float32)]
    psum x2, waiting for transfers between devices: 52.1 us -> 99.5 us  [the longest x1 53.5 us: per_device(): lax.psum(dot_f32(attn, wo), 'model')]
    all_to_all x0 -> x2, waiting for transfers between devices: none -> 33.8 us  [the longest x1 17.9 us: per_device(): lax.all_to_all(k_all, 'model', 0, 0, tiled=False)]
    dot_general x3 -> x1, local copies, waits for them, and re-layouts: 33.3 us -> 0.07 us  [per_device(): jnp.einsum('bs,bsd->bd', last_sel, prompt, preferred_element_type=jnp.flo...]
    convert_element_type x2, local copies, waits for them, and re-layouts: 35.2 us -> 2.27 us  [the longest x1 2.24 us: per_device(): jnp.einsum('bsd,jdh->jsbh', normed, wv_full, preferred_element_type=jnp.f...]
    transpose x2 -> x0, local copies, waits for them, and re-layouts: 30.3 us -> none  [per_device(): jnp.moveaxis(lax.dynamic_slice_in_dim(val_blocks, my_idx * kv_loc, kv_loc...]
    convert_element_type x2 -> x1, other arithmetic: 22.5 us -> 1.18 us  [rms_norm(): (hid_f32 * inv_rms * gain_vec.astype(jnp.float32)).astype(jnp.bfloat16)]
  transfers between devices with their start and end apart: 11 -> 6, of which waited for: 9 -> 5; matrix products, arithmetic and copies ran while one was open for 34% -> 26% of each run, Pallas kernels for 0% -> 0%
where the time goes in v1:
time: 304 us; the launch traced here: 303 us
  waiting for transfers between devices  139 us (46%)
  matrix products  54.8 us (18%)
  blocking collectives  38.6 us (13%)
  local copies, waits for them, and re-layouts  24.8 us (8%)
  other arithmetic  21.9 us (7%)
  between operations  14.2 us (5%)
  starting transfers between devices  9.92 us (3%)
    psum x1, waiting for transfers between devices, per_device(): lax.psum(dot_f32(attn, wo), 'model')  53.5 us
    psum x1, waiting for transfers between devices, per_device(): lax.psum(dot_f32(mid, wd), 'model')  46.1 us
    psum x1, blocking collectives, per_device(): last_row = lax.psum(last_row, 'model').astype(jnp.bfloat16)  38.6 us
    all_to_all x1, waiting for transfers between devices, per_device(): lax.all_to_all(k_all, 'model', 0, 0, tiled=False)  17.9 us
    dot_general x6, matrix products, dot_f32(): return jnp.dot(a, b, preferred_element_type=jnp.float32)  16.3 us
    all_to_all x1, waiting for transfers between devices, per_device(): lax.all_to_all(v_all, 'model', 0, 0, tiled=False)  16 us
    dot_general x1, matrix products, per_device(): jnp.einsum('bsd,jdh->jsbh', normed, wk_full, preferred_element_type=jnp.f...  14.4 us
    dot_general x1, matrix products, per_device(): jnp.einsum('bsd,jdh->jsbh', normed, wv_full, preferred_element_type=jnp.f...  14.2 us
  transfers between devices with their start and end apart: 6, of which 5 were waited for; matrix products, arithmetic and copies ran while one was open for 26% of the time, Pallas kernels for 0%

profile of v1, /device:TPU:112, one launch (start us, length us, event | category | flops | bytes accessed | tf_op | source)
XLA Modules:
  0.0 303.1 jit_solution(15865260663517618219)
XLA Ops:
  7.2 0.0 copy-start
  7.2 0.1 all-gather.5.cloned.1.call-start
  7.3 0.7 all-gather.5.cloned.1.call-update
  8.0 0.1 all-gather.3.cloned.1.call-start
  8.1 0.7 all-gather.3.cloned.1.call-update
  8.8 1.2 fusion.104
  10.1 0.5 copy-done.14
  10.6 0.1 compare_bitcast_fusion
  10.7 5.1 %fusion.84 = f32[32,1,3072]{2,1,0:T(1,128)S(1)} fusion(bf16[32,48,3072]{2,1,0:T(8,128)(2,1)} %param.12, pred[32,48,1]{1,0,2:T(32,128)(4,1)S(1)} %compare_bitcast_fusion), kind=kOutput, calls=%fused_computation.81 | convolution fusion | flops 9437184 | bytes 9831936 | tf_op jit(solution)/shard_map/bs,bsd->bd/dot_general | solution.py:60
  15.7 0.1 copy.56
  15.8 38.6 %all-reduce.7 = bf16[32,3072]{1,0:T(8,128)(2,1)S(1)} all-reduce(f32[32,3072]{1,0:T(8,128)S(1)} %bitcast.117), channel_id=1, replica_groups=mesh['replica'=2,'model'=8] {'model'}, use_global_device_ids=true, to_apply=%region_0.0 | all-reduce | flops 98304 | bytes 589824 | tf_op jit(solution)/shard_map/psum | solution.py:61
  54.5 0.2 fusion.55
  54.7 0.5 add_rsqrt_fusion.2
  55.2 5.6 %fusion.1 = f32[32,48]{1,0:T(8,128)S(1)} fusion(bf16[32,48,3072]{2,1,0:T(8,128)(2,1)} %param.12), kind=kLoop, calls=%fused_computation.3 | loop fusion | flops 14154240 | bytes 9443328 | tf_op jit(solution)/shard_map/reduce_sum | solution.py:12
  60.8 0.2 multiply_cosine_fusion.1
  60.9 0.0 all-gather.5.cloned.1.call-done
  61.0 14.4 %fusion.21 = f32[8,48,32,128]{3,1,0,2:T(8,128)S(1)} fusion(bf16[8,3072,128]{2,1,0:T(8,128)(2,1)} %all-gather.5.cloned.1.call-done, bf16[32,48,3072]{2,1,0:T(8,128)(2,1)} %param.12, f32[3072]{0:T(1024)S(1)} %bitcast.123, f32[32,48]{1,0:T(8,128)S(1)} %add_rsqrt_fusion), kind=kOutput, calls=%fused_computation.27 | convolution fusion | flops 9682550784 | bytes 22038528 | tf_op jit(solution)/shard_map/bsd,jdh->jsbh/dot_general | solution.py:54
  75.4 2.3 subtract_convert_fusion
  77.7 1.8 pad_maximum_fusion.2
  79.5 2.2 copy.37
  81.8 4.8 %all-to-all-start.1 = ((bf16[8,48,32,128]{3,1,2,0:T(8,128)(2,1)}), bf16[8,48,32,128]{3,1,2,0:T(8,128)(2,1)}, u32[]{:S(2)}, u32[]{:S(2)}) async-start(bf16[8,48,32,128]{3,1,2,0:T(8,128)(2,1)} %copy.37), calls=%async_computation.1 | async-start | bytes 6291456 | tf_op jit(solution)/shard_map/all_to_all | solution.py:57
  86.6 3.9 %all-gather.3.cloned.1.call-done = bf16[8,3072,128]{2,1,0:T(8,128)(2,1)} async-done(((bf16[1,3072,128]{2,1,0:T(8,128)(2,1)}), bf16[8,3072,128]{2,1,0:T(8,128)(2,1)}) %all-gather.3.cloned.1.call-update) | async-done | bytes 6291472 | tf_op jit(solution)/shard_map/all_gather | solution.py:52
  90.5 14.2 %convert_bitcast_fusion = bf16[8,48,32,128]{3,1,0,2:T(8,128)(2,1)S(1)} fusion(bf16[8,3072,128]{2,1,0:T(8,128)(2,1)} %all-gather.3.cloned.1.call-done, bf16[32,48,3072]{2,1,0:T(8,128)(2,1)} %param.12, f32[3072]{0:T(1024)S(1)} %bitcast.124, f32[32,48]{1,0:T(8,128)S(1)} %add_rsqrt_fusion), kind=kOutput, calls=%fused_computation.26 | convolution fusion | flops 9684123648 | bytes 18892800 | tf_op jit(solution)/shard_map/bsd,jdh->jsbh/dot_general | solution.py:55
  104.7 0.0 copy-start.3
  104.7 2.2 copy.31
  106.9 17.9 %all-to-all-done.1 = bf16[8,48,32,128]{3,1,2,0:T(8,128)(2,1)} async-done(((bf16[8,48,32,128]{3,1,2,0:T(8,128)(2,1)}), bf16[8,48,32,128]{3,1,2,0:T(8,128)(2,1)}, u32[]{:S(2)}, u32[]{:S(2)}) %all-to-all-start.1) | async-done | bytes 3145760 | tf_op jit(solution)/shard_map/all_to_all | solution.py:57
  124.8 4.6 %all-to-all-start = ((bf16[8,48,32,128]{3,1,2,0:T(8,128)(2,1)}), bf16[8,48,32,128]{3,1,2,0:T(8,128)(2,1)}, u32[]{:S(2)}, u32[]{:S(2)}) async-start(bf16[8,48,32,128]{3,1,2,0:T(8,128)(2,1)} %copy.31), calls=%async_computation | async-start | bytes 6291456 | tf_op jit(solution)/shard_map/all_to_all | solution.py:58
  129.4 0.1 all-reduce.4.cloned.1.call-start
  129.5 1.2 fusion.57
  130.7 0.2 convolution_bitcast_fusion
  130.9 0.0 copy-start.4
  131.0 0.9 fusion.97
  131.8 0.1 pad_maximum_fusion.6
  131.9 4.3 %copy.34 = bf16[1,3072,384]{1,2,0:T(8,128)(2,1)} copy(bf16[1,3072,384]{2,1,0:T(8,128)(2,1)} %param.16) | data formatting | bytes 4718592 | tf_op args[4]
  136.2 0.7 add_convert_fusion.2
  136.9 0.9 multiply_cosine_fusion
  137.8 2.5 fusion.67
  140.3 0.1 subtract_convert_fusion.1
  140.4 0.7 copy.35
  141.1 0.7 copy.36
  141.8 0.2 fusion.54
  142.1 0.9 iota_compare_fusion
  142.9 0.2 pad_add_fusion
  143.1 4.4 %copy.38 = bf16[8,48,32,128]{3,1,0,2:T(8,128)(2,1)} copy(bf16[8,48,32,128]{3,1,2,0:T(8,128)(2,1)} %all-to-all-done.1) | data formatting | bytes 6291456 | tf_op jit(solution)/shard_map/all_to_all | solution.py:57
  147.6 4.1 %fusion.105 = (f32[32,2,3]{2,1,0:T(2,128)S(1)}, f32[32,2,3,385]{3,2,1,0:T(4,128)}) fusion(bf16[1,32,128]{2,0,1:T(2,128)(2,1)S(1)} %copy.39, bf16[384,32,128]{2,0,1:T(8,128)(2,1)} %bitcast.112, pred[32,2,385]{2,1,0:T(4,128)(4,1)S(1)} %pad_add_fusion, bf16[2,32,3,64]{3,2,0,1:T(4,128)(2,1)S(1)} %copy-done.10, bf16[2,32,3,64]{3,2,0,1:T(4,128)(2,1)S(1)} %copy-done.9), kind=kOutput, calls=%fused_computation.117 | convolution fusion | flops 25625728 | bytes 3524160 | tf_op jit(solution)/shard_map/sub | solution.py:77
  151.7 16.0 %all-to-all-done = bf16[8,48,32,128]{3,1,2,0:T(8,128)(2,1)} async-done(((bf16[8,48,32,128]{3,1,2,0:T(8,128)(2,1)}), bf16[8,48,32,128]{3,1,2,0:T(8,128)(2,1)}, u32[]{:S(2)}, u32[]{:S(2)}) %all-to-all-start) | async-done | bytes 3145760 | tf_op jit(solution)/shard_map/all_to_all | solution.py:58
  167.6 2.8 copy.32
  170.5 1.7 copy-done.1
  172.1 0.7 fusion.51
  172.9 1.4 fusion.26
  174.4 0.1 all-reduce.4.cloned.1.call-update
  174.4 0.3 all-reduce.6.cloned.1.call-start
  174.8 53.5 %all-reduce.4.cloned.1.call-done = f32[64,3072]{1,0:T(8,128)} async-done(((f32[64,3072]{1,0:T(8,128)}), f32[64,3072]{1,0:T(8,128)}) %all-reduce.4.cloned.1.call-update) | async-done | bytes 786448 | tf_op jit(solution)/shard_map/psum | solution.py:80
  228.3 1.3 fusion.59
  229.6 4.0 %fusion.9 = f32[64,1024]{1,0:T(8,128)S(1)} fusion(bf16[1,3072,1024]{2,1,0:T(8,128)(2,1)} %param.21, bf16[64,3072]{1,0:T(8,128)(2,1)S(1)} %get-tuple-element.17, f32[3072]{0:T(1024)S(1)} %bitcast.121, f32[64]{0:T(128)S(1)} %add_rsqrt_fusion.1), kind=kOutput, calls=%fused_computation.11 | convolution fusion | flops 403439616 | bytes 6959360 | tf_op jit(solution)/shard_map/dot_general | solution.py:28
  233.7 7.9 %fusion.5 = f32[64,3072]{1,0:T(8,128)} fusion(bf16[1,1024,3072]{2,1,0:T(8,128)(2,1)} %param.23, bf16[1,3072,1024]{2,1,0:T(8,128)(2,1)} %param.22, f32[64,1024]{1,0:T(8,128)S(1)} %fusion.9, bf16[64,3072]{1,0:T(8,128)(2,1)S(1)} %get-tuple-element.17, f32[3072]{0:T(1024)S(1)} %bitcast.122, f32[64]{0:T(128)S(1)} %add_rsqrt_fusion.1), kind=kOutput, calls=%fused_computation.7 | convolution fusion | flops 806486016 | bytes 14037248 | tf_op jit(solution)/shard_map/dot_general | solution.py:28
  241.6 0.1 all-reduce.6.cloned.1.call-update
  241.6 2.3 fusion.32
  243.9 2.1 copy.41
  246.1 0.2 fusion.33
  246.3 2.1 copy.42
  248.5 46.1 %all-reduce.6.cloned.1.call-done = f32[64,3072]{1,0:T(8,128)} async-done(((f32[64,3072]{1,0:T(8,128)}), f32[64,3072]{1,0:T(8,128)}) %all-reduce.6.cloned.1.call-update) | async-done | bytes 786448 | tf_op jit(solution)/shard_map/psum | solution.py:83
  294.5 1.2 fusion.62
  295.7 0.8 fusion.103
  (37 shorter events, 0.2 us)
Async XLA Ops:
  7.2 165.8 %copy-start = (bf16[1,384,3072]{2,1,0:T(8,128)(2,1)S(1)}, bf16[1,384,3072]{2,1,0:T(8,128)(2,1)}, u32[]{:S(2)}) copy-start(bf16[1,384,3072]{2,1,0:T(8,128)(2,1)} %param.19) | copy-start | bytes 7077892
  7.2 53.8 %all-gather.5.cloned.1.call-start = ((), (), s32[]{:S(2)}) async-start(), calls=%async_computation.3 | async-start | bytes 7077888 | tf_op jit(solution)/shard_map/all_gather | solution.py:51
  8.0 82.5 %all-gather.3.cloned.1.call-start = ((), (), s32[]{:S(2)}) async-start(), calls=%async_computation.2 | async-start | bytes 7077888 | tf_op jit(solution)/shard_map/all_gather | solution.py:52
  10.1 0.5 copy-start.14
  10.7 5.1 %copy-start.11 = (bf16[1,3072]{1,0:T(2,128)(2,1)S(1)}, bf16[1,3072]{1,0:T(2,128)(2,1)}, u32[]{:S(2)}) copy-start(bf16[1,3072]{1,0:T(2,128)(2,1)} %param.15) | copy-start | bytes 18436
  10.7 43.8 %copy-start.7 = (bf16[32,3072]{1,0:T(8,128)(2,1)S(1)}, bf16[32,3072]{1,0:T(8,128)(2,1)}, u32[]{:S(2)}) copy-start(bf16[32,3072]{1,0:T(8,128)(2,1)} %param.14) | copy-start | bytes 589828
  54.4 20.9 %copy-start.5 = (bf16[32,3072]{1,0:T(8,128)(2,1)}, bf16[32,3072]{1,0:T(8,128)(2,1)S(1)}, u32[]{:S(2)}) copy-start(bf16[32,3072]{1,0:T(8,128)(2,1)S(1)} %all-reduce.7) | copy-start | bytes 589828
  54.6 76.3 %copy-start.13 = (f32[64]{0:T(128)}, f32[64]{0:T(128)S(1)}, u32[]{:S(2)}) copy-start(f32[64]{0:T(128)S(1)} %multiply_power_fusion) | copy-start | bytes 772
  81.8 43.0 %all-to-all-start.1 = ((bf16[8,48,32,128]{3,1,2,0:T(8,128)(2,1)}), bf16[8,48,32,128]{3,1,2,0:T(8,128)(2,1)}, u32[]{:S(2)}, u32[]{:S(2)}) async-start(bf16[8,48,32,128]{3,1,2,0:T(8,128)(2,1)} %copy.37), calls=%async_computation.1 | async-start | bytes 6291456 | tf_op jit(solution)/shard_map/all_to_all | solution.py:57
  104.7 26.0 %copy-start.3 = (bf16[1,3072,128]{2,1,0:T(8,128)(2,1)S(1)}, bf16[1,3072,128]{2,1,0:T(8,128)(2,1)}, u32[]{:S(2)}) copy-start(bf16[1,3072,128]{2,1,0:T(8,128)(2,1)} %param.17) | copy-start | bytes 2359300
  124.8 42.8 %all-to-all-start = ((bf16[8,48,32,128]{3,1,2,0:T(8,128)(2,1)}), bf16[8,48,32,128]{3,1,2,0:T(8,128)(2,1)}, u32[]{:S(2)}, u32[]{:S(2)}) async-start(bf16[8,48,32,128]{3,1,2,0:T(8,128)(2,1)} %copy.31), calls=%async_computation | async-start | bytes 6291456 | tf_op jit(solution)/shard_map/all_to_all | solution.py:58
  129.4 98.8 %all-reduce.4.cloned.1.call-start = ((), (), s32[]{:S(2)}) async-start(), calls=%async_computation.4 | async-start | bytes 1572864 | tf_op jit(solution)/shard_map/psum | solution.py:80
  130.9 10.8 %copy-start.4 = (bf16[1,3072,128]{2,1,0:T(8,128)(2,1)S(1)}, bf16[1,3072,128]{2,1,0:T(8,128)(2,1)}, u32[]{:S(2)}) copy-start(bf16[1,3072,128]{2,1,0:T(8,128)(2,1)} %param.18) | copy-start | bytes 2359300
  142.0 5.6 %copy-start.9 = (bf16[2,32,3,64]{3,2,0,1:T(4,128)(2,1)S(1)}, bf16[2,32,3,64]{3,2,0,1:T(4,128)(2,1)}, u32[]{:S(2)}) copy-start(bf16[2,32,3,64]{3,2,0,1:T(4,128)(2,1)} %copy.35) | copy-start | bytes 73732
  142.0 5.5 %copy-start.10 = (bf16[2,32,3,64]{3,2,0,1:T(4,128)(2,1)S(1)}, bf16[2,32,3,64]{3,2,0,1:T(4,128)(2,1)}, u32[]{:S(2)}) copy-start(bf16[2,32,3,64]{3,2,0,1:T(4,128)(2,1)} %copy.36) | copy-start | bytes 73732
  167.6 4.5 %copy-start.15 = (f32[32,2,3,385]{3,2,1,0:T(4,128)S(1)}, f32[32,2,3,385]{3,2,1,0:T(4,128)}, u32[]{:S(2)}) copy-start(f32[32,2,3,385]{3,2,1,0:T(4,128)} %get-tuple-element.35) | copy-start | bytes 887044
  170.5 1.7 copy-start.1
  172.1 2.6 copy-start.12
  172.1 56.1 %copy-start.6 = (bf16[32,3072]{1,0:T(8,128)(2,1)S(1)}, bf16[32,3072]{1,0:T(8,128)(2,1)}, u32[]{:S(2)}) copy-start(bf16[32,3072]{1,0:T(8,128)(2,1)} %copy-done.5) | copy-start | bytes 589828
  172.1 56.1 %copy-start.8 = (bf16[32,3072]{1,0:T(8,128)(2,1)S(1)}, bf16[32,3072]{1,0:T(8,128)(2,1)}, u32[]{:S(2)}) copy-start(bf16[32,3072]{1,0:T(8,128)(2,1)} %param.14) | copy-start | bytes 589828
  174.4 120.1 %all-reduce.6.cloned.1.call-start = ((), (), s32[]{:S(2)}) async-start(), calls=%async_computation.5 | async-start | bytes 1572864 | tf_op jit(solution)/shard_map/psum | solution.py:83
  241.6 4.5 %copy-start.2 = (bf16[8,48,32,128]{3,1,0,2:T(8,128)(2,1)S(1)}, bf16[8,48,32,128]{3,1,0,2:T(8,128)(2,1)}, u32[]{:S(2)}) copy-start(bf16[8,48,32,128]{3,1,0,2:T(8,128)(2,1)} %copy-done.1) | copy-start | bytes 9437188
Sparse Core Ops, SparseCore 0:
  9.6 43.0 all-gather.4
  54.3 36.1 all-gather.2
  174.6 53.6 all-reduce.3
  241.7 52.7 all-reduce.5

commit v2 on v1

v2 whole, which is shorter than its diff:
```python
import functools

import jax
import jax.numpy as jnp
from jax import lax
from jax.experimental import pallas as pl
from jax.experimental.pallas import tpu as pltpu
from jax.sharding import PartitionSpec as P

HEAD_DIM = 128
NEG_BIG = -1e30
CORES = 2
MESH_ID = pl.DeviceIdType.MESH
BF16 = jnp.bfloat16
F32 = jnp.float32


def dot_f32(a, b):
    return jnp.dot(a, b, preferred_element_type=F32)


def dot_bt(a, b):
    return lax.dot_general(a, b, (((1,), (1,)), ((), ())), preferred_element_type=F32)


def norm_rows(x_f32, gain_f32):
    inv_rms = lax.rsqrt(jnp.mean(x_f32 * x_f32, axis=-1, keepdims=True) + 1e-5)
    return x_f32 * inv_rms * gain_f32


def rotate(x_f32, cos_full, sin_signed):
    return x_f32 * cos_full + pltpu.roll(x_f32, HEAD_DIM // 2, 1) * sin_signed


def kernel(n_dev, n_batch, seq_loc, d_model, heads_loc, ff_loc,
           lens, prompt, new_tok, g_attn, g_mlp, cos_pos, sin_pos, cos_row, sin_row, len_row,
           wq, wk, wv, wo, wg, wu, wd,
           last_out, dec_out, kout, vout,
           xbuf, normed, wbuf, stage, kvrecv, relay, wq_v, wg_v, wu_v, res_k, res_v,
           last_f, xl_own, xl_sib, xl_sum, xl_recv, xl_half, xl_oth, rows_f, rows_n, q_s, knew, vnew,
           m_s, l_s, acc_s, part, d2d_in, rs_sum, rs_in, agbuf, x1_f, hid_n, part2, d2d_in2, rs_sum2, rs_in2, agbuf2,
           xsem, ldsem, w_send, w_recv, kv_send, kv_recv, rl_recv, xl_send, xl_rsem, out_sem, ar_send, ar_recv, ag_send, ag_recv):
    n_chip = n_dev // CORES
    n_tok = n_batch * seq_loc
    n_row = 2 * n_batch
    piece = n_row // n_dev
    half = d_model // 2
    me = lax.axis_index('model')
    c = me // CORES
    k = me % CORES
    o_core = 1 - k

    def dev(rel, kk):
        chip = lax.rem(c + rel, n_chip)
        return CORES * chip + (k if kk == 0 else o_core)

    RIGHT, OPP, LEFT = 1, 2, 3

    def slot(rel, kk):
        return rel * CORES + kk

    def rcopy(src, dst, ssem, rsem, target):
        return pltpu.make_async_remote_copy(src_ref=src, dst_ref=dst, send_sem=ssem, recv_sem=rsem,
                                            device_id={'model': target}, device_id_type=MESH_ID)

    own_w = slot(0, 0)
    ld_wk = pltpu.make_async_copy(wk, wbuf.at[own_w, :, pl.ds(0, HEAD_DIM)], ldsem.at[0])
    ld_wv = pltpu.make_async_copy(wv, wbuf.at[own_w, :, pl.ds(HEAD_DIM, HEAD_DIM)], ldsem.at[1])
    ld_wk.start()
    ld_wv.start()
    n_x = xbuf.shape[0]

    def x_copy(b, s):
        return pltpu.make_async_copy(prompt.at[b], xbuf.at[s], xsem.at[s])

    for b in range(n_x - 1):
        x_copy(b, b).start()

    barrier = pltpu.get_barrier_semaphore()
    for d in range(1, n_dev):
        pl.semaphore_signal(barrier, inc=1, device_id={'model': lax.rem(me + d, n_dev)}, device_id_type=MESH_ID)
    pl.semaphore_wait(barrier, n_dev - 1)

    def w_half(sl, h):
        return wbuf.at[sl, pl.ds(h * half, half), :]

    def w_copy(n, src_slot, dst_slot, h, target):
        return rcopy(w_half(src_slot, h), w_half(dst_slot, h), w_send.at[n], w_recv.at[dst_slot * 2 + h], target)

    ld_wk.wait()
    ld_wv.wait()
    sends = []
    to_r = [w_copy(0, own_w, slot(LEFT, 0), 0, dev(RIGHT, 0)), w_copy(1, own_w, slot(LEFT, 0), 1, dev(RIGHT, 0))]
    to_l = [w_copy(2, own_w, slot(RIGHT, 0), 1, dev(LEFT, 0)), w_copy(3, own_w, slot(RIGHT, 0), 0, dev(LEFT, 0))]
    to_s = [w_copy(4, own_w, slot(0, 1), 0, dev(0, 1)), w_copy(5, own_w, slot(0, 1), 1, dev(0, 1))]
    for cp in (to_r[0], to_l[0], to_r[1], to_l[1], to_s[0], to_s[1]):
        cp.start()
        sends.append(cp)
    fwd_r = w_copy(6, slot(LEFT, 0), slot(OPP, 0), 0, dev(RIGHT, 0))
    fwd_l = w_copy(7, slot(RIGHT, 0), slot(OPP, 0), 1, dev(LEFT, 0))
    sib_fwd = {}
    n = 8
    for rel in (LEFT, RIGHT, OPP):
        for h in range(2):
            sib_fwd[rel, h] = w_copy(n, slot(rel, 0), slot(rel, 1), h, dev(0, 1))
            n += 1

    ld_wq = pltpu.make_async_copy(wq, wq_v, ldsem.at[2])
    ld_wg = pltpu.make_async_copy(wg, wg_v, ldsem.at[3])
    ld_wu = pltpu.make_async_copy(wu, wu_v, ldsem.at[4])

    gain = g_attn[...].astype(F32)
    pos0 = me * seq_loc

    @pl.loop(0, n_batch)
    def _(b):
        s = lax.rem(b, n_x)

        @pl.when(b + n_x - 1 < n_batch)
        def _():
            x_copy(b + n_x - 1, lax.rem(b + n_x - 1, n_x)).start()

        x_copy(b, s).wait()
        x = xbuf[s].astype(F32)
        normed[pl.ds(pl.multiple_of(b * seq_loc, seq_loc), seq_loc), :] = norm_rows(x, gain).astype(BF16)
        here = (lax.broadcasted_iota(jnp.int32, (seq_loc, 1), 0) + pos0 == lens[b] - 1).astype(F32)
        last_f[pl.ds(b, 1), :] = jnp.sum(x * here, axis=0, keepdims=True)

    ld_wq.start()
    ld_wg.start()
    ld_wu.start()

    xl_own[...] = last_f[...].astype(BF16)
    xl_a = rcopy(xl_own, xl_sib, xl_send.at[0], xl_rsem.at[0], dev(0, 1))
    xl_a.start()

    def head(sl, dst):
        for_rows = 512

        @pl.loop(0, n_tok // for_rows)
        def _(m):
            r0 = pl.multiple_of(m * for_rows, for_rows)
            res = dot_f32(normed[pl.ds(r0, for_rows), :], wbuf[sl])
            res_k[pl.ds(r0, for_rows), :] = res[:, :HEAD_DIM]
            res_v[pl.ds(r0, for_rows), :] = res[:, HEAD_DIM:]

        @pl.loop(0, seq_loc, unroll=4)
        def _(s):
            rows = pl.ds(pl.multiple_of(s * n_batch, n_batch), n_batch)
            kt = res_k[pl.ds(s, n_batch, stride=seq_loc), :]
            dst[0, rows, :] = rotate(kt, cos_pos[pl.ds(s, 1), :], sin_pos[pl.ds(s, 1), :]).astype(BF16)
            dst[1, rows, :] = res_v[pl.ds(s, n_batch, stride=seq_loc), :].astype(BF16)

    def kv_slot_at_receiver(rel, kk):
        return slot((n_chip - rel) % n_chip, kk)

    def kv_copy(n, rel, kk):
        sl = kv_slot_at_receiver(rel, kk)
        return rcopy(stage.at[slot(rel, kk) - 1], kvrecv.at[sl], kv_send.at[n], kv_recv.at[sl], dev(rel, kk))

    head(own_w, kvrecv.at[own_w])

    def wait_w(rel, kk, h):
        w_copy(0, slot(rel, kk), slot(rel, kk), h, dev(0, 1)).wait_recv()

    wait_w(0, 1, 0)
    wait_w(0, 1, 1)
    head(slot(0, 1), stage.at[slot(0, 1) - 1])
    kv_sib = kv_copy(0, 0, 1)
    kv_sib.start()
    sends.append(kv_sib)

    hb = n_batch // CORES
    xl_a.wait_recv()
    my_rows = pl.ds(pl.multiple_of(k * hb, hb), hb)
    xl_sum[...] = xl_own[my_rows, :] + xl_sib[my_rows, :]
    xl_b = [rcopy(xl_sum, xl_recv.at[n_chip - 1 - rel], xl_send.at[rel], xl_rsem.at[n_chip - rel], dev(rel, 0)) for rel in (RIGHT, LEFT, OPP)]
    for cp in xl_b:
        cp.start()
    sends.append(xl_a)
    sends.extend(xl_b)

    wait_w(LEFT, 0, 0)
    fwd_r.start()
    sib_fwd[LEFT, 0].start()
    wait_w(RIGHT, 0, 1)
    fwd_l.start()
    sib_fwd[RIGHT, 1].start()
    sends += [fwd_r, fwd_l]
    wait_w(LEFT, 0, 1)
    sib_fwd[LEFT, 1].start()
    wait_w(RIGHT, 0, 0)
    sib_fwd[RIGHT, 0].start()
    n = 1
    kv_nb = {}
    for kk in range(2):
        for rel in (RIGHT, LEFT):
            if kk == 1:
                wait_w(rel, 1, 0)
                wait_w(rel, 1, 1)
            head(slot(rel, kk), stage.at[slot(rel, kk) - 1])
            kv_nb[rel, kk] = kv_copy(n, rel, kk)
            kv_nb[rel, kk].start()
            sends.append(kv_nb[rel, kk])
            n += 1
        if kk == 0:
            for cp in xl_b:
                cp.wait_recv()
            xl_half[...] = xl_sum[...] + xl_recv[0] + (xl_recv[1] + xl_recv[2])
            xl_c = rcopy(xl_half, xl_oth, xl_send.at[4], xl_rsem.at[4], dev(0, 1))
            xl_c.start()
            sends.append(xl_c)
    wait_w(OPP, 0, 0)
    sib_fwd[OPP, 0].start()
    wait_w(OPP, 0, 1)
    sib_fwd[OPP, 1].start()
    sends += list(sib_fwd.values())

    def relay_in(n, part_i, kk):
        return rcopy(stage.at[slot(OPP, kk) - 1, part_i], relay.at[part_i, kk], kv_send.at[n], rl_recv.at[part_i * 2 + kk],
                     dev(RIGHT if part_i == 0 else LEFT, 0))

    def relay_out(n, part_i, kk):
        sl = slot(OPP, kk)
        return rcopy(relay.at[part_i, kk], kvrecv.at[sl, part_i], kv_send.at[n], rl_recv.at[4 + part_i * 2 + kk],
                     dev(RIGHT if part_i == 0 else LEFT, kk))

    r_in = {}
    for kk in range(2):
        if kk == 1:
            wait_w(OPP, 1, 0)
            wait_w(OPP, 1, 1)
        head(slot(OPP, kk), stage.at[slot(OPP, kk) - 1])
        for p in range(2):
            r_in[p, kk] = relay_in(n, p, kk)
            r_in[p, kk].start()
            sends.append(r_in[p, kk])
            n += 1
    r_out = {(p, kk): relay_out(5 + 4 + p * 2 + kk, p, kk) for kk in range(2) for p in range(2)}

    wd_v = normed.at[pl.ds(0, ff_loc), :]
    wo_v = normed.at[pl.ds(ff_loc, heads_loc * HEAD_DIM), :]
    ld_wo = pltpu.make_async_copy(wo, wo_v, ldsem.at[0])
    ld_wd = pltpu.make_async_copy(wd, wd_v, ldsem.at[1])
    ld_wo.start()
    ld_wd.start()

    xl_c.wait_recv()
    oth_rows = pl.ds(pl.multiple_of(o_core * hb, hb), hb)
    rows_f[my_rows, :] = xl_half[...].astype(F32)
    rows_f[oth_rows, :] = xl_oth[...].astype(F32)
    rows_f[pl.ds(n_batch, n_batch), :] = new_tok[...].astype(F32)
    rows_n[...] = norm_rows(rows_f[...], gain).astype(BF16)
    ld_wq.wait()
    q_all = dot_f32(rows_n[...], wq_v[...])
    for g in range(heads_loc):
        q_g = rotate(q_all[:, g * HEAD_DIM:(g + 1) * HEAD_DIM], cos_row[...], sin_row[...])
        q_s[pl.ds(g * n_row, n_row), :] = q_g.astype(BF16)
    kv_new = dot_f32(rows_n[...], wbuf[own_w])
    new_rows = slice(n_batch, n_row)
    k_new = rotate(kv_new[new_rows, :HEAD_DIM], cos_row[pl.ds(n_batch, n_batch), :], sin_row[pl.ds(n_batch, n_batch), :])
    knew[...] = k_new.astype(BF16)
    vnew[...] = kv_new[new_rows, HEAD_DIM:].astype(BF16)
    tail_row = n_dev * n_tok
    outs = [pltpu.make_async_copy(knew, kout.at[pl.ds(tail_row, n_batch), :], out_sem.at[0]),
            pltpu.make_async_copy(vnew, vout.at[pl.ds(tail_row, n_batch), :], out_sem.at[1])]
    for cp in outs:
        cp.start()

    scale = HEAD_DIM ** -0.5
    n_q = heads_loc * n_row
    chunk = min(512, n_tok)
    m_s[...] = jnp.full(m_s.shape, NEG_BIG, F32)
    l_s[...] = jnp.zeros(l_s.shape, F32)
    acc_s[...] = jnp.zeros(acc_s.shape, F32)

    def update(sc, valid, v_blk):
        sc = jnp.where(valid, sc * scale, NEG_BIG)
        m_old = m_s[...]
        m_new = jnp.maximum(m_old, jnp.max(sc, axis=-1, keepdims=True))
        prob = jnp.where(valid, jnp.exp(sc - m_new), 0.0)
        alpha = jnp.exp(m_old - m_new)
        l_s[...] = l_s[...] * alpha + jnp.sum(prob, axis=-1, keepdims=True)
        acc_s[...] = acc_s[...] * alpha + dot_f32(prob.astype(BF16), v_blk)
        m_s[...] = m_new

    def attend(sl, src):
        @pl.loop(0, n_tok // chunk)
        def _(ch):
            rows = pl.ds(pl.multiple_of(ch * chunk, chunk), chunk)
            sc = dot_bt(q_s[...], kvrecv[sl, 0, rows, :])
            col = lax.broadcasted_iota(jnp.int32, (n_q, chunk), 1)
            row = lax.broadcasted_iota(jnp.int32, (n_q, chunk), 0)
            pos = src * seq_loc + ch * (chunk // n_batch) + col // n_batch
            valid = (col % n_batch == row % n_batch) & (pos < len_row[...])
            update(sc, valid, kvrecv[sl, 1, rows, :])

    def put_out(n, sl, src):
        rows = pl.ds(pl.multiple_of(src * n_tok, n_tok), n_tok)
        for i, ref in enumerate((kout, vout)):
            cp = pltpu.make_async_copy(kvrecv.at[sl, i], ref.at[rows, :], out_sem.at[2 + 2 * n + i])
            cp.start()
            outs.append(cp)

    col = lax.broadcasted_iota(jnp.int32, (n_q, n_batch), 1)
    row = lax.broadcasted_iota(jnp.int32, (n_q, n_batch), 0)
    is_new = (row // n_batch) % 2 == 1
    update(dot_bt(q_s[...], knew[...]), (col == row % n_batch) & is_new, vnew[...])
    put_out(0, own_w, me)
    attend(own_w, me)
    kv_sib.wait_recv()
    put_out(1, slot(0, 1), dev(0, 1))
    attend(slot(0, 1), dev(0, 1))
    n = 2
    for kk in range(2):
        for rel in (RIGHT, LEFT):
            src_rel = (n_chip - rel) % n_chip
            kv_nb[rel, kk].wait_recv()
            put_out(n, slot(src_rel, kk), dev(src_rel, kk))
            attend(slot(src_rel, kk), dev(src_rel, kk))
            n += 1
    for kk in range(2):
        for p in range(2):
            r_in[p, kk].wait_recv()
            r_out[p, kk].start()
            sends.append(r_out[p, kk])
    for kk in range(2):
        for p in range(2):
            r_out[p, kk].wait_recv()
        put_out(n, slot(OPP, kk), dev(OPP, kk))
        attend(slot(OPP, kk), dev(OPP, kk))
        n += 1
    o_all = (acc_s[...] / l_s[...]).astype(BF16)

    def sum_over_model(i, part_r, d2d_r, sum_r, in_r):
        cp = rcopy(part_r.at[o_core], d2d_r, ar_send.at[4 * i], ar_recv.at[4 * i], dev(0, 1))
        cp.start()
        cp.wait_recv()
        sends.append(cp)
        cps = []
        for rel in (OPP, RIGHT, LEFT):
            chip = lax.rem(c + rel, n_chip)
            sum_r[rel] = part_r[k, chip] + d2d_r[chip]
            cps.append(rcopy(sum_r.at[rel], in_r.at[n_chip - 1 - rel], ar_send.at[4 * i + rel], ar_recv.at[4 * i + n_chip - rel], dev(rel, 0)))
            cps[-1].start()
        total = part_r[k, c] + d2d_r[c]
        for cp in cps[1:] + cps[:1]:
            cp.wait_recv()
        sends.extend(cps)
        return total + in_r[0] + in_r[2] + in_r[1]

    def gather_rows(i, buf):
        cps = []
        for rel in (OPP, RIGHT, LEFT):
            cps.append(rcopy(buf.at[k, c], buf.at[k, c], ag_send.at[8 * i + rel], ag_recv.at[8 * i + n_chip - rel], dev(rel, 0)))
        cps.append(rcopy(buf.at[k, c], buf.at[k, c], ag_send.at[8 * i], ag_recv.at[8 * i], dev(0, 1)))
        for cp in cps:
            cp.start()
        fw = []
        for rel, cp in ((LEFT, cps[1]), (RIGHT, cps[2]), (OPP, cps[0])):
            cp.wait_recv()
            chip = lax.rem(c + rel, n_chip)
            f = rcopy(buf.at[k, chip], buf.at[k, chip], ag_send.at[8 * i + 4 + rel], ag_recv.at[8 * i + 4 + rel], dev(0, 1))
            f.start()
            fw.append(f)
        for cp in [cps[3]] + fw:
            cp.wait_recv()
        sends.extend(cps + fw)

    ld_wo.wait()
    o_rows = jnp.concatenate([o_all[g * n_row:(g + 1) * n_row] for g in range(heads_loc)], axis=1)
    for p in range(n_dev):
        r = slice(p * piece, (p + 1) * piece)
        if p == 0:
            o_out = dot_f32(o_rows, wo_v[...])
        part[p // n_chip, p % n_chip] = o_out[r]
    my_piece = pl.ds(pl.multiple_of((k * n_chip + c) * piece, piece), piece)
    att_sum = sum_over_model(0, part, d2d_in, rs_sum, rs_in)
    x1 = (rows_f[my_piece, :] + att_sum).astype(BF16).astype(F32)
    x1_f[...] = x1
    agbuf[k, c] = norm_rows(x1, g_mlp[...].astype(F32)).astype(BF16)
    gather_rows(0, agbuf)
    for p in range(0, n_dev, 2):
        two = [agbuf[i // n_chip, i % n_chip].astype(F32) for i in (p, p + 1)]
        hid_n[pl.ds(p * piece, 2 * piece), :] = jnp.concatenate(two, axis=0).astype(BF16)
    ld_wg.wait()
    ld_wu.wait()
    gate = dot_f32(hid_n[...], wg_v[...])
    up = dot_f32(hid_n[...], wu_v[...])
    mid = (gate * jax.nn.sigmoid(gate) * up).astype(BF16)
    ld_wd.wait()
    down = dot_f32(mid, wd_v[...])
    for p in range(n_dev):
        part2[p // n_chip, p % n_chip] = down[p * piece:(p + 1) * piece]
    mlp_sum = sum_over_model(1, part2, d2d_in2, rs_sum2, rs_in2)
    agbuf2[k, c] = (x1_f[...] + mlp_sum).astype(BF16)
    gather_rows(1, agbuf2)
    for p in range(0, n_dev, 2):
        two = jnp.concatenate([agbuf2[i // n_chip, i % n_chip].astype(F32) for i in (p, p + 1)], axis=0).astype(BF16)
        ref, r0 = (last_out, p * piece) if p * piece < n_batch else (dec_out, p * piece - n_batch)
        ref[pl.ds(r0, 2 * piece), :] = two
    for cp in sends:
        cp.wait_send()
    for cp in outs:
        cp.wait()


def solution(mesh):
    n_dev = mesh.shape['model']
    assert n_dev == 4 * CORES
    seq_spec = P('replica', 'model', None)
    col_spec = P(None, None, 'model')
    row_spec = P(None, 'model', None)
    gain_spec = P(None, None)
    tok_spec = P('replica', None)
    cache_spec = P(None, 'replica', None, 'model', None)
    in_specs = (seq_spec, P('replica'), tok_spec, gain_spec, col_spec, col_spec, col_spec, row_spec, gain_spec, col_spec, col_spec, row_spec)
    out_specs = (tok_spec, tok_spec, cache_spec, cache_spec)

    def tables(positions):
        half_dim = HEAD_DIM // 2
        inv_freq = 10000.0 ** (-2.0 * jnp.arange(half_dim, dtype=F32) / HEAD_DIM)
        angles = positions.astype(F32)[:, None] * inv_freq
        cos_tab, sin_tab = jnp.cos(angles), jnp.sin(angles)
        return jnp.concatenate([cos_tab, cos_tab], axis=1), jnp.concatenate([-sin_tab, sin_tab], axis=1)

    def per_device(prompt, lengths, new_tok, norm_attn, w_q, w_k, w_v, w_o, norm_mlp, w_gate, w_up, w_down):
        assert w_q.shape[0] == 1 and w_k.shape[2] == HEAD_DIM
        n_batch, seq_loc, d_model = prompt.shape
        n_tok = n_batch * seq_loc
        heads_loc = w_q.shape[2] // HEAD_DIM
        ff_loc = w_gate.shape[2]
        n_row = 2 * n_batch
        piece = n_row // n_dev
        n_chip = n_dev // CORES
        hb = n_batch // CORES
        n_q = heads_loc * n_row
        cos_pos, sin_pos = tables(lax.axis_index('model') * seq_loc + jnp.arange(seq_loc))
        cos_row, sin_row = tables(jnp.concatenate([lengths - 1, lengths]))
        len_row = jnp.tile(lengths, 2 * heads_loc)[:, None]
        vm = pl.BlockSpec(memory_space=pltpu.VMEM)
        hbm = pl.BlockSpec(memory_space=pl.ANY)
        V = pltpu.VMEM
        DMA = pltpu.SemaphoreType.DMA
        slab = (2, n_tok, HEAD_DIM)
        wide = (CORES, n_chip, piece, d_model)
        scratch = [
            V((4, seq_loc, d_model), BF16), V((n_tok, d_model), BF16), V((n_dev, d_model, 2 * HEAD_DIM), BF16),
            V((n_dev - 1,) + slab, BF16), V((n_dev,) + slab, BF16), V((2, 2, n_tok, HEAD_DIM), BF16),
            V((d_model, heads_loc * HEAD_DIM), BF16), V((d_model, ff_loc), BF16), V((d_model, ff_loc), BF16),
            V((n_tok, HEAD_DIM), F32), V((n_tok, HEAD_DIM), F32),
            V((n_batch, d_model), F32), V((n_batch, d_model), BF16), V((n_batch, d_model), BF16), V((hb, d_model), BF16),
            V((n_chip - 1, hb, d_model), BF16), V((hb, d_model), BF16), V((hb, d_model), BF16),
            V((n_row, d_model), F32), V((n_row, d_model), BF16), V((n_q, HEAD_DIM), BF16),
            V((n_batch, HEAD_DIM), BF16), V((n_batch, HEAD_DIM), BF16),
            V((n_q, 1), F32), V((n_q, 1), F32), V((n_q, HEAD_DIM), F32),
            V(wide, F32), V(wide[1:], F32), V(wide[1:], F32), V((n_chip - 1,) + wide[2:], F32), V(wide, BF16), V(wide[2:], F32),
            V((n_row, d_model), BF16),
            V(wide, F32), V(wide[1:], F32), V(wide[1:], F32), V((n_chip - 1,) + wide[2:], F32), V(wide, BF16),
            DMA((4,)), DMA((5,)), DMA((14,)), DMA((4 * n_dev,)), DMA((13,)), DMA((n_dev,)), DMA((8,)), DMA((5,)), DMA((5,)),
            DMA((2 + 2 * n_dev,)), DMA((8,)), DMA((8,)), DMA((16,)), DMA((16,)),
        ]
        cache = jax.ShapeDtypeStruct(((seq_loc * n_dev + 1) * n_batch, HEAD_DIM), BF16)
        tok = jax.ShapeDtypeStruct((n_batch, d_model), BF16)
        last, dec, kc, vc = pl.pallas_call(
            functools.partial(kernel, n_dev, n_batch, seq_loc, d_model, heads_loc, ff_loc),
            out_shape=[tok, tok, cache, cache],
            in_specs=[pl.BlockSpec(memory_space=pltpu.SMEM), hbm] + [vm] * 8 + [hbm] * 7,
            out_specs=[vm, vm, hbm, hbm],
            scratch_shapes=scratch,
            compiler_params=pltpu.CompilerParams(collective_id=0, has_side_effects=True, vmem_limit_bytes=67_043_328),
        )(lengths, prompt, new_tok, norm_attn, norm_mlp, cos_pos, sin_pos, cos_row, sin_row, len_row,
          w_q[0], w_k[0], w_v[0], w_o[0], w_gate[0], w_up[0], w_down[0])

        def as_cache(arr):
            return jnp.transpose(arr.reshape(1, seq_loc * n_dev + 1, 1, n_batch, HEAD_DIM), (0, 3, 1, 2, 4))

        return dec, last, as_cache(kc), as_cache(vc)

    return jax.shard_map(per_device, mesh=mesh, in_specs=in_specs, out_specs=out_specs, check_vma=False)
```

time: 304 us -> 179 us (0.59)
  Pallas kernels: 0 us -> 164 us
  waiting for transfers between devices: 139 us -> 0 us
  matrix products: 54.8 us -> 0 us
  blocking collectives: 38.6 us -> 0 us
  other arithmetic: 21.9 us -> 3.18 us
  local copies, waits for them, and re-layouts: 24.8 us -> 10.6 us
  between operations: 14.2 us -> 0.67 us
  starting transfers between devices: 9.92 us -> 0 us
    pallas_call x0 -> x1, Pallas kernels: none -> 164 us  [per_device(): pl.pallas_call(functools.partial(kernel, n_dev, n_batch, seq_loc, d_model...]
    psum x2 -> x0, waiting for transfers between devices: 99.5 us -> none  [the longest x1 53.5 us: per_device(): lax.psum(dot_f32(attn, wo), 'model')]
    dot_general x10 -> x0, matrix products: 50.7 us -> none  [the longest x6 16.3 us: dot_f32(): return jnp.dot(a, b, preferred_element_type=jnp.float32)]
    psum x1 -> x0, blocking collectives: 38.6 us -> none  [per_device(): last_row = lax.psum(last_row, 'model').astype(jnp.bfloat16)]
    all_to_all x2 -> x0, waiting for transfers between devices: 33.8 us -> none  [the longest x1 17.9 us: per_device(): lax.all_to_all(k_all, 'model', 0, 0, tiled=False)]
    all_to_all x2 -> x0, starting transfers between devices: 9.45 us -> none  [the longest x1 4.82 us: per_device(): lax.all_to_all(k_all, 'model', 0, 0, tiled=False)]
    all_to_all x2 -> x0, local copies, waits for them, and re-layouts: 7.26 us -> none  [the longest x1 4.44 us: per_device(): lax.all_to_all(k_all, 'model', 0, 0, tiled=False)]
    reduce_sum x3 -> x0, other arithmetic: 7.11 us -> none  [rms_norm(): jnp.mean(hid_f32 * hid_f32, axis=-1, keepdims=True) + 1e-05]
  transfers between devices with their start and end apart: 6 -> 0, of which waited for: 5 -> 0; matrix products, arithmetic and copies ran while one was open for 26% -> 0% of each run, Pallas kernels for 0% -> 0%
where the time goes in v2:
time: 179 us; the launch traced here: 178 us
  Pallas kernels  164 us (92%)
  local copies, waits for them, and re-layouts  10.6 us (6%)
  other arithmetic  3.18 us (2%)
    pallas_call x1, Pallas kernels, per_device(): pl.pallas_call(functools.partial(kernel, n_dev, n_batch, seq_loc, d_model...  164 us
    unnamed x6, local copies, waits for them, and re-layouts  9.15 us

profile of v2, /device:TPU:112, one launch (start us, length us, event | category | flops | bytes accessed | tf_op | source)
XLA Modules:
  0.0 178.0 jit_solution(15912207903296116485)
XLA Ops:
  0.7 0.7 broadcast_add_fusion
  1.3 0.7 add_convert_fusion
  2.1 0.7 tile.2
  2.7 0.2 fusion.1
  2.9 0.7 pad_maximum_fusion.2
  3.6 0.8 broadcast_in_dim_tile.4.len_row
  4.3 0.2 fusion
  4.5 0.7 pad_maximum_fusion
  5.2 163.6 %shard_map.147 = (bf16[32,3072]{1,0:T(8,128)(2,1)}, bf16[32,3072]{1,0:T(8,128)(2,1)}, bf16[12320,128]{1,0:T(8,128)(2,1)}, bf16[12320,128]{1,0:T(8,128)(2,1)}) custom-call(s32[32]{0:T(128)} %lens.1, bf16[32,48,3072]{2,1,0:T(8,128)(2,1)} %prompt.1, bf16[32,3072]{1,0:T(8,128)(2,1)} %new_tok.1, bf16[1,3072]{1,0:T(2,128)(2,1)} %g_attn.1, bf16[1,3072]{1,0:T(2,128)(2,1)} %g_mlp.1, ...), custom_call_target="tpu_custom_call" | custom-call | tf_op jit(solution)/shard_map/pallas_call | solution.py:465
  168.8 1.6 copy.25
  170.5 1.6 copy.26
  172.1 0.0 copy-start
  172.1 4.2 %copy.27 = bf16[1,32,385,1,128]{4,1,3,2,0:T(8,128)(2,1)} copy(bf16[1,32,385,1,128]{4,1,3,2,0:T(8,128)(2,1)} %bitcast.21) | data formatting | bytes 6307840
  176.3 0.0 copy-done
  176.3 1.7 copy.28
  (2 shorter events, 0.0 us)
Async XLA Ops:
  172.1 4.3 %copy-start = (bf16[12320,128]{1,0:T(8,128)(2,1)S(1)}, bf16[12320,128]{1,0:T(8,128)(2,1)}, u32[]{:S(2)}) copy-start(bf16[12320,128]{1,0:T(8,128)(2,1)} %get-tuple-element.11) | copy-start | bytes 9461764

commit v3 on v2

v3 whole, which is shorter than its diff:
```python
import functools
import math

import jax
import jax.numpy as jnp
from jax import lax
from jax.experimental import pallas as pl
from jax.experimental.pallas import tpu as pltpu
from jax.sharding import PartitionSpec as P

HEAD_DIM = 128
NEG_BIG = -1e30
CORES = 2
N_BULK = 2
PLAN = (2, 1, 3, 1, 1)
MESH_ID = pl.DeviceIdType.MESH
BF16 = jnp.bfloat16
F32 = jnp.float32


def dot_f32(a, b):
    return jnp.dot(a, b, preferred_element_type=F32)


def dot_bt(a, b):
    return lax.dot_general(a, b, (((1,), (1,)), ((), ())), preferred_element_type=F32)


def norm_rows(x_f32, gain_f32):
    inv_rms = lax.rsqrt(jnp.mean(x_f32 * x_f32, axis=-1, keepdims=True) + 1e-5)
    return x_f32 * inv_rms * gain_f32


def rotate(x_f32, cos_full, sin_signed):
    return x_f32 * cos_full + pltpu.roll(x_f32, HEAD_DIM // 2, 1) * sin_signed


def kernel(n_dev, n_batch, seq_loc, d_model, heads_loc, ff_loc, n_bulk, plan,
           lens, prompt, new_tok, g_attn, g_mlp, wq, wk, wv, wo, wg, wu, wd,
           last_out, dec_out, kout, vout,
           xbuf, normed, wbuf, stage, kvrecv, wq_v, wg_v, wu_v, res_k, res_v,
           len_v, cos_pos, sin_pos, cos_row, sin_row,
           last_f, xl_own, xl_sib, xl_sum, xl_recv, xl_half, xl_oth, rows_f, rows_n, q_s, q_in, knew, vnew,
           m_s, l_s, acc_s, m_p, l_p, acc_p, msg, msg_in,
           part, d2d_in, rs_sum, rs_in, agbuf, x1_f, hid_n, part2, d2d_in2, rs_sum2, rs_in2, agbuf2,
           xsem, ldsem, w_send, w_recv, kv_send, kv_recv, bulk_send, bulk_recv, pt_send, pt_recv, xl_send, xl_rsem, out_sem,
           ar_send, ar_recv, ag_send, ag_recv):
    n_chip = n_dev // CORES
    n_tok = n_batch * seq_loc
    n_row = 2 * n_batch
    piece = n_row // n_dev
    half = d_model // 2
    me = lax.axis_index('model')
    c = me // CORES
    k = me % CORES
    o_core = 1 - k

    def dev(rel, kk):
        chip = lax.rem(c + rel, n_chip)
        return CORES * chip + (k if kk == 0 else o_core)

    RIGHT, OPP, LEFT = 1, 2, 3

    def slot(rel, kk):
        return rel * CORES + kk

    def rcopy(src, dst, ssem, rsem, target):
        return pltpu.make_async_remote_copy(src_ref=src, dst_ref=dst, send_sem=ssem, recv_sem=rsem,
                                            device_id={'model': target}, device_id_type=MESH_ID)

    own_w = slot(0, 0)
    ld_wk = pltpu.make_async_copy(wk, wbuf.at[own_w, :, pl.ds(0, HEAD_DIM)], ldsem.at[0])
    ld_wv = pltpu.make_async_copy(wv, wbuf.at[own_w, :, pl.ds(HEAD_DIM, HEAD_DIM)], ldsem.at[1])
    ld_wk.start()
    ld_wv.start()
    n_x = xbuf.shape[0]

    def x_copy(b, s):
        return pltpu.make_async_copy(prompt.at[b], xbuf.at[s], xsem.at[s])

    for b in range(n_x - 1):
        x_copy(b, b).start()

    barrier = pltpu.get_barrier_semaphore()
    for d in range(1, n_dev):
        pl.semaphore_signal(barrier, inc=1, device_id={'model': lax.rem(me + d, n_dev)}, device_id_type=MESH_ID)
    pl.semaphore_wait(barrier, n_dev - 1)

    def w_half(sl, h):
        return wbuf.at[sl, pl.ds(h * half, half), :]

    def w_copy(n, src_slot, dst_slot, h, target):
        return rcopy(w_half(src_slot, h), w_half(dst_slot, h), w_send.at[n], w_recv.at[dst_slot * 2 + h], target)

    ld_wk.wait()
    ld_wv.wait()
    sends = []

    def go(cp):
        cp.start()
        sends.append(cp)
        return cp

    to_r = [w_copy(0, own_w, slot(LEFT, 0), 0, dev(RIGHT, 0)), w_copy(1, own_w, slot(LEFT, 0), 1, dev(RIGHT, 0))]
    to_l = [w_copy(2, own_w, slot(RIGHT, 0), 1, dev(LEFT, 0)), w_copy(3, own_w, slot(RIGHT, 0), 0, dev(LEFT, 0))]
    to_s = [w_copy(4, own_w, slot(0, 1), 0, dev(0, 1)), w_copy(5, own_w, slot(0, 1), 1, dev(0, 1))]
    for cp in (to_r[0], to_l[0], to_s[0], to_s[1]):
        go(cp)
    fwd_r = w_copy(6, slot(LEFT, 0), slot(OPP, 0), 0, dev(RIGHT, 0))
    fwd_l = w_copy(7, slot(RIGHT, 0), slot(OPP, 0), 1, dev(LEFT, 0))
    sib_fwd = {}
    n = 8
    for rel in (LEFT, RIGHT, OPP):
        for h in range(2):
            sib_fwd[rel, h] = w_copy(n, slot(rel, 0), slot(rel, 1), h, dev(0, 1))
            n += 1

    ld_wq = pltpu.make_async_copy(wq, wq_v, ldsem.at[2])
    ld_wg = pltpu.make_async_copy(wg, wg_v, ldsem.at[3])
    ld_wu = pltpu.make_async_copy(wu, wu_v, ldsem.at[4])

    gain = g_attn[...].astype(F32)
    pos0 = me * seq_loc

    @pl.loop(0, n_batch)
    def _(b):
        s = lax.rem(b, n_x)

        @pl.when(b + n_x - 1 < n_batch)
        def _():
            x_copy(b + n_x - 1, lax.rem(b + n_x - 1, n_x)).start()

        x_copy(b, s).wait()
        x = xbuf[s].astype(F32)
        normed[pl.ds(pl.multiple_of(b * seq_loc, seq_loc), seq_loc), :] = norm_rows(x, gain).astype(BF16)
        here = (lax.broadcasted_iota(jnp.int32, (seq_loc, 1), 0) + pos0 == lens[b] - 1).astype(F32)
        last_f[pl.ds(b, 1), :] = jnp.sum(x * here, axis=0, keepdims=True)
        len_v[pl.ds(b, 1), :] = jnp.full((1, HEAD_DIM), lens[b], jnp.int32)

    ld_wq.start()
    ld_wg.start()
    ld_wu.start()

    xl_own[...] = last_f[...].astype(BF16)
    xl_a = go(rcopy(xl_own, xl_sib, xl_send.at[0], xl_rsem.at[0], dev(0, 1)))

    def table(cos_ref, sin_ref, rows, pos):
        lane = lax.broadcasted_iota(jnp.int32, pos.shape, 1)
        hd = HEAD_DIM // 2
        step = jnp.where(lane < hd, lane, lane - hd).astype(F32)
        angle = pos.astype(F32) * jnp.exp(step * (-2.0 * math.log(10000.0) / HEAD_DIM))
        cos_ref[rows, :] = jnp.cos(angle)
        sin_ref[rows, :] = jnp.where(lane < hd, -1.0, 1.0) * jnp.sin(angle)

    table(cos_pos, sin_pos, pl.ds(0, seq_loc), lax.broadcasted_iota(jnp.int32, (seq_loc, HEAD_DIM), 0) + pos0)
    table(cos_row, sin_row, pl.ds(0, n_batch), len_v[...] - 1)
    table(cos_row, sin_row, pl.ds(n_batch, n_batch), len_v[...])

    hb = n_batch // CORES
    xl_a.wait_recv()
    my_rows = pl.ds(pl.multiple_of(k * hb, hb), hb)
    oth_rows = pl.ds(pl.multiple_of(o_core * hb, hb), hb)
    xl_sum[...] = xl_own[my_rows, :] + xl_sib[my_rows, :]
    xl_b = [go(rcopy(xl_sum, xl_recv.at[n_chip - 1 - rel], xl_send.at[rel], xl_rsem.at[n_chip - rel], dev(rel, 0))) for rel in (RIGHT, LEFT, OPP)]
    go(to_r[1])
    go(to_l[1])

    def head(sl, dst):
        for_rows = 512

        @pl.loop(0, n_tok // for_rows)
        def _(m):
            r0 = pl.multiple_of(m * for_rows, for_rows)
            res = dot_f32(normed[pl.ds(r0, for_rows), :], wbuf[sl])
            res_k[pl.ds(r0, for_rows), :] = res[:, :HEAD_DIM]
            res_v[pl.ds(r0, for_rows), :] = res[:, HEAD_DIM:]

        @pl.loop(0, seq_loc, unroll=4)
        def _(s):
            rows = pl.ds(pl.multiple_of(s * n_batch, n_batch), n_batch)
            kt = res_k[pl.ds(s, n_batch, stride=seq_loc), :]
            dst[0, rows, :] = rotate(kt, cos_pos[pl.ds(s, 1), :], sin_pos[pl.ds(s, 1), :]).astype(BF16)
            dst[1, rows, :] = res_v[pl.ds(s, n_batch, stride=seq_loc), :].astype(BF16)

    def kv_copy(n, rel, kk):
        sl = slot((n_chip - rel) % n_chip, kk)
        return rcopy(stage.at[slot(rel, kk) - 1], kvrecv.at[sl], kv_send.at[n], kv_recv.at[sl], dev(rel, kk))

    def wait_w(rel, kk, h):
        w_copy(0, slot(rel, kk), slot(rel, kk), h, dev(0, 1)).wait_recv()

    head(own_w, kvrecv.at[own_w])
    wait_w(0, 1, 0)
    wait_w(0, 1, 1)
    head(slot(0, 1), stage.at[slot(0, 1) - 1])
    kv_sib = go(kv_copy(0, 0, 1))

    wait_w(LEFT, 0, 0)
    go(fwd_r)
    go(sib_fwd[LEFT, 0])
    wait_w(RIGHT, 0, 1)
    go(fwd_l)
    go(sib_fwd[RIGHT, 1])
    for cp in xl_b:
        cp.wait_recv()
    xl_half[...] = xl_sum[...] + xl_recv[0] + (xl_recv[1] + xl_recv[2])
    xl_c = go(rcopy(xl_half, xl_oth, xl_send.at[4], xl_rsem.at[4], dev(0, 1)))

    rows_f[my_rows, :] = xl_half[...].astype(F32)
    rows_f[pl.ds(n_batch, n_batch), :] = new_tok[...].astype(F32)
    ld_wq.wait()
    xl_c.wait_recv()
    rows_f[oth_rows, :] = xl_oth[...].astype(F32)
    rows_n[...] = norm_rows(rows_f[...], gain).astype(BF16)
    q_all = dot_f32(rows_n[...], wq_v[...])
    for g in range(heads_loc):
        q_g = rotate(q_all[:, g * HEAD_DIM:(g + 1) * HEAD_DIM], cos_row[...], sin_row[...])
        q_s[pl.ds(g * n_row, n_row), :] = q_g.astype(BF16)
    q_out = [go(rcopy(q_s, q_in.at[kk], pt_send.at[kk], pt_recv.at[kk], dev(OPP, kk))) for kk in range(2)]
    kv_new = dot_f32(rows_n[...], wbuf[own_w])
    new_rows = slice(n_batch, n_row)
    k_new = rotate(kv_new[new_rows, :HEAD_DIM], cos_row[pl.ds(n_batch, n_batch), :], sin_row[pl.ds(n_batch, n_batch), :])
    knew[...] = k_new.astype(BF16)
    vnew[...] = kv_new[new_rows, HEAD_DIM:].astype(BF16)
    tail_row = n_dev * n_tok
    outs = [pltpu.make_async_copy(knew, kout.at[pl.ds(tail_row, n_batch), :], out_sem.at[0]),
            pltpu.make_async_copy(vnew, vout.at[pl.ds(tail_row, n_batch), :], out_sem.at[1])]
    for cp in outs:
        cp.start()

    wait_w(LEFT, 0, 1)
    go(sib_fwd[LEFT, 1])
    wait_w(RIGHT, 0, 0)
    go(sib_fwd[RIGHT, 0])
    n = 1
    kv_nb = {}
    for kk in range(2):
        for rel in (RIGHT, LEFT):
            if kk == 1:
                wait_w(rel, 1, 0)
                wait_w(rel, 1, 1)
            head(slot(rel, kk), stage.at[slot(rel, kk) - 1])
            kv_nb[rel, kk] = go(kv_copy(n, rel, kk))
            n += 1
    wait_w(OPP, 0, 0)
    go(sib_fwd[OPP, 0])
    wait_w(OPP, 0, 1)
    go(sib_fwd[OPP, 1])

    scale = HEAD_DIM ** -0.5
    n_q = heads_loc * n_row
    chunk = min(512, n_tok)
    mine = (m_s, l_s, acc_s)

    def reset(state):
        state[0][...] = jnp.full(state[0].shape, NEG_BIG, F32)
        state[1][...] = jnp.zeros(state[1].shape, F32)
        state[2][...] = jnp.zeros(state[2].shape, F32)

    def update(state, sc, valid, v_blk):
        m_r, l_r, acc_r = state
        sc = jnp.where(valid, sc * scale, NEG_BIG)
        m_old = m_r[...]
        m_new = jnp.maximum(m_old, jnp.max(sc, axis=-1, keepdims=True))
        prob = jnp.where(valid, jnp.exp(sc - m_new), 0.0)
        alpha = jnp.exp(m_old - m_new)
        l_r[...] = l_r[...] * alpha + jnp.sum(prob, axis=-1, keepdims=True)
        acc_r[...] = acc_r[...] * alpha + dot_f32(prob.astype(BF16), v_blk)
        m_r[...] = m_new

    def attend(state, q_ref, kv_ref, src):
        @pl.loop(0, n_tok // chunk)
        def _(ch):
            rows = pl.ds(pl.multiple_of(ch * chunk, chunk), chunk)
            sc = dot_bt(q_ref[...], kv_ref[0, rows, :])
            col = lax.broadcasted_iota(jnp.int32, (n_q, chunk), 1)
            row = lax.broadcasted_iota(jnp.int32, (n_q, chunk), 0)
            pos = src * seq_loc + ch * (chunk // n_batch) + col // n_batch
            len_row = jnp.concatenate([len_v[:, :1]] * (n_q // n_batch), axis=0)
            valid = (col % n_batch == row % n_batch) & (pos < len_row)
            update(state, sc, valid, kv_ref[1, rows, :])

    lane_rows = [(i, min(HEAD_DIM, n_q - i)) for i in range(0, n_q, HEAD_DIM)]

    def on_diag(size):
        return lax.broadcasted_iota(jnp.int32, (size, HEAD_DIM), 0) == lax.broadcasted_iota(jnp.int32, (size, HEAD_DIM), 1)

    def put_column(ref, r0, column):
        for j, (i, size) in enumerate(lane_rows):
            ref[pl.ds(r0 + j, 1), :] = jnp.sum(jnp.where(on_diag(size), column[i:i + size], 0.0), axis=0, keepdims=True)

    def get_column(ref, r0):
        cols = [jnp.sum(jnp.where(on_diag(size), ref[pl.ds(r0 + j, 1), :], 0.0), axis=1, keepdims=True) for j, (i, size) in enumerate(lane_rows)]
        return jnp.concatenate(cols, axis=0)

    n_lr = len(lane_rows)
    pt_out = []
    for kk in range(2):
        if kk == 1:
            wait_w(OPP, 1, 0)
            wait_w(OPP, 1, 1)
        block = stage.at[slot(OPP, kk) - 1]
        head(slot(OPP, kk), block)
        q_out[kk].wait_recv()
        other = (m_p, l_p, acc_p)
        reset(other)
        attend(other, q_in.at[kk], block, me)
        msg[kk, pl.ds(0, n_q), :] = acc_p[...]
        put_column(msg.at[kk], n_q, m_p[...])
        put_column(msg.at[kk], n_q + n_lr, l_p[...])
        pt_out.append(go(rcopy(msg.at[kk], msg_in.at[kk], pt_send.at[2 + kk], pt_recv.at[2 + kk], dev(OPP, kk))))

    per = n_tok // n_bulk
    bulk = []
    for kk in range(2):
        for i in range(2):
            for j in range(n_bulk):
                rows = pl.ds(j * per, per)
                x = len(bulk)
                bulk.append(rcopy(stage.at[slot(OPP, kk) - 1, i, rows, :], kvrecv.at[slot(OPP, kk), i, rows, :], bulk_send.at[x], bulk_recv.at[x], dev(OPP, kk)))
    waiting = list(bulk)

    def send_bulk(count):
        for _ in range(count):
            if waiting:
                go(waiting.pop(0))

    send_bulk(plan[0])

    wd_v = normed.at[pl.ds(0, ff_loc), :]
    wo_v = normed.at[pl.ds(ff_loc, heads_loc * HEAD_DIM), :]
    ld_wo = pltpu.make_async_copy(wo, wo_v, ldsem.at[0])
    ld_wd = pltpu.make_async_copy(wd, wd_v, ldsem.at[1])
    ld_wo.start()
    ld_wd.start()

    def put_out(n, sl, src):
        rows = pl.ds(pl.multiple_of(src * n_tok, n_tok), n_tok)
        for i, ref in enumerate((kout, vout)):
            cp = pltpu.make_async_copy(kvrecv.at[sl, i], ref.at[rows, :], out_sem.at[2 + 2 * n + i])
            cp.start()
            outs.append(cp)

    reset(mine)
    col = lax.broadcasted_iota(jnp.int32, (n_q, n_batch), 1)
    row = lax.broadcasted_iota(jnp.int32, (n_q, n_batch), 0)
    is_new = (row // n_batch) % 2 == 1
    update(mine, dot_bt(q_s[...], knew[...]), (col == row % n_batch) & is_new, vnew[...])
    put_out(0, own_w, me)
    attend(mine, q_s, kvrecv.at[own_w], me)
    kv_sib.wait_recv()
    put_out(1, slot(0, 1), dev(0, 1))
    attend(mine, q_s, kvrecv.at[slot(0, 1)], dev(0, 1))
    n = 2
    for kk in range(2):
        for rel in (RIGHT, LEFT):
            src_rel = (n_chip - rel) % n_chip
            kv_nb[rel, kk].wait_recv()
            put_out(n, slot(src_rel, kk), dev(src_rel, kk))
            attend(mine, q_s, kvrecv.at[slot(src_rel, kk)], dev(src_rel, kk))
            n += 1
    for kk in range(2):
        pt_out[kk].wait_recv()
        m_o = get_column(msg_in.at[kk], n_q)
        l_o = get_column(msg_in.at[kk], n_q + n_lr)
        m_old = m_s[...]
        m_new = jnp.maximum(m_old, m_o)
        f_mine, f_oth = jnp.exp(m_old - m_new), jnp.exp(m_o - m_new)
        l_s[...] = l_s[...] * f_mine + l_o * f_oth
        acc_s[...] = acc_s[...] * f_mine + msg_in[kk, pl.ds(0, n_q), :] * f_oth
        m_s[...] = m_new
    o_all = (acc_s[...] / l_s[...]).astype(BF16)

    def sum_over_model(i, part_r, d2d_r, sum_r, in_r):
        cp = go(rcopy(part_r.at[o_core], d2d_r, ar_send.at[4 * i], ar_recv.at[4 * i], dev(0, 1)))
        cp.wait_recv()
        cps = []
        for rel in (OPP, RIGHT, LEFT):
            chip = lax.rem(c + rel, n_chip)
            sum_r[rel] = part_r[k, chip] + d2d_r[chip]
            cps.append(go(rcopy(sum_r.at[rel], in_r.at[n_chip - 1 - rel], ar_send.at[4 * i + rel], ar_recv.at[4 * i + n_chip - rel], dev(rel, 0))))
        send_bulk(plan[1 + 2 * i])
        total = part_r[k, c] + d2d_r[c]
        for cp in cps[1:] + cps[:1]:
            cp.wait_recv()
        return total + in_r[0] + in_r[2] + in_r[1]

    def gather_rows(i, buf):
        cps = []
        for rel in (OPP, RIGHT, LEFT):
            cps.append(go(rcopy(buf.at[k, c], buf.at[k, c], ag_send.at[8 * i + rel], ag_recv.at[8 * i + n_chip - rel], dev(rel, 0))))
        cps.append(go(rcopy(buf.at[k, c], buf.at[k, c], ag_send.at[8 * i], ag_recv.at[8 * i], dev(0, 1))))
        send_bulk(plan[2 + 2 * i])
        fw = []
        for rel, cp in ((LEFT, cps[1]), (RIGHT, cps[2]), (OPP, cps[0])):
            cp.wait_recv()
            chip = lax.rem(c + rel, n_chip)
            fw.append(go(rcopy(buf.at[k, chip], buf.at[k, chip], ag_send.at[8 * i + 4 + rel], ag_recv.at[8 * i + 4 + rel], dev(0, 1))))
        for cp in [cps[3]] + fw:
            cp.wait_recv()

    ld_wo.wait()
    o_rows = jnp.concatenate([o_all[g * n_row:(g + 1) * n_row] for g in range(heads_loc)], axis=1)
    o_out = dot_f32(o_rows, wo_v[...])
    for p in range(n_dev):
        part[p // n_chip, p % n_chip] = o_out[p * piece:(p + 1) * piece]
    my_piece = pl.ds(pl.multiple_of((k * n_chip + c) * piece, piece), piece)
    att_sum = sum_over_model(0, part, d2d_in, rs_sum, rs_in)
    x1 = (rows_f[my_piece, :] + att_sum).astype(BF16).astype(F32)
    x1_f[...] = x1
    agbuf[k, c] = norm_rows(x1, g_mlp[...].astype(F32)).astype(BF16)
    gather_rows(0, agbuf)
    for p in range(0, n_dev, 2):
        two = [agbuf[i // n_chip, i % n_chip].astype(F32) for i in (p, p + 1)]
        hid_n[pl.ds(p * piece, 2 * piece), :] = jnp.concatenate(two, axis=0).astype(BF16)
    ld_wg.wait()
    ld_wu.wait()
    gate = dot_f32(hid_n[...], wg_v[...])
    up = dot_f32(hid_n[...], wu_v[...])
    mid = (gate * jax.nn.sigmoid(gate) * up).astype(BF16)
    ld_wd.wait()
    down = dot_f32(mid, wd_v[...])
    for p in range(n_dev):
        part2[p // n_chip, p % n_chip] = down[p * piece:(p + 1) * piece]
    mlp_sum = sum_over_model(1, part2, d2d_in2, rs_sum2, rs_in2)
    agbuf2[k, c] = (x1_f[...] + mlp_sum).astype(BF16)
    gather_rows(1, agbuf2)
    send_bulk(len(waiting))
    for p in range(0, n_dev, 2):
        two = jnp.concatenate([agbuf2[i // n_chip, i % n_chip].astype(F32) for i in (p, p + 1)], axis=0).astype(BF16)
        ref, r0 = (last_out, p * piece) if p * piece < n_batch else (dec_out, p * piece - n_batch)
        ref[pl.ds(r0, 2 * piece), :] = two
    for kk in range(2):
        for cp in bulk[kk * 2 * n_bulk:(kk + 1) * 2 * n_bulk]:
            cp.wait_recv()
        put_out(n, slot(OPP, kk), dev(OPP, kk))
        n += 1
    for cp in sends:
        cp.wait_send()
    for cp in outs:
        cp.wait()


def write_kernel(n_part, last_in, dec_in, k_in, v_in, last_out, dec_out, k_out, v_out, tok_v, kv_v, in_sem, out_sem):
    rows = k_in.shape[0] // n_part
    pairs = [(last_in, last_out, tok_v.at[0]), (dec_in, dec_out, tok_v.at[1])]
    for p in range(n_part):
        for i, (src, dst) in enumerate(((k_in, k_out), (v_in, v_out))):
            r = pl.ds(p * rows, rows)
            pairs.append((src.at[r, :], dst.at[r, :], kv_v.at[i, r, :]))
    loads = [pltpu.make_async_copy(src, buf, in_sem.at[n]) for n, (src, dst, buf) in enumerate(pairs)]
    stores = [pltpu.make_async_copy(buf, dst, out_sem.at[n]) for n, (src, dst, buf) in enumerate(pairs)]
    for cp in loads:
        cp.start()
    for ld, st in zip(loads, stores):
        ld.wait()
        st.start()
    for cp in stores:
        cp.wait()


def solution(mesh):
    n_dev = mesh.shape['model']
    assert n_dev == 4 * CORES
    seq_spec = P('replica', 'model', None)
    col_spec = P(None, None, 'model')
    row_spec = P(None, 'model', None)
    gain_spec = P(None, None)
    tok_spec = P('replica', None)
    cache_spec = P(None, 'replica', None, 'model', None)
    in_specs = (seq_spec, P('replica'), tok_spec, gain_spec, col_spec, col_spec, col_spec, row_spec, gain_spec, col_spec, col_spec, row_spec)
    out_specs = (tok_spec, tok_spec, cache_spec, cache_spec)

    def per_device(prompt, lengths, new_tok, norm_attn, w_q, w_k, w_v, w_o, norm_mlp, w_gate, w_up, w_down):
        assert w_q.shape[0] == 1 and w_k.shape[2] == HEAD_DIM
        n_batch, seq_loc, d_model = prompt.shape
        n_tok = n_batch * seq_loc
        heads_loc = w_q.shape[2] // HEAD_DIM
        ff_loc = w_gate.shape[2]
        n_row = 2 * n_batch
        piece = n_row // n_dev
        n_chip = n_dev // CORES
        hb = n_batch // CORES
        n_q = heads_loc * n_row
        vm = pl.BlockSpec(memory_space=pltpu.VMEM)
        hbm = pl.BlockSpec(memory_space=pl.ANY)
        V = pltpu.VMEM
        DMA = pltpu.SemaphoreType.DMA
        slab = (2, n_tok, HEAD_DIM)
        wide = (CORES, n_chip, piece, d_model)
        n_lr = 2 * pl.cdiv(n_q, HEAD_DIM)
        state = [V((n_q, 1), F32), V((n_q, 1), F32), V((n_q, HEAD_DIM), F32)]
        note = V((2, pl.cdiv(n_q + n_lr, 8) * 8, HEAD_DIM), F32)
        scratch = [
            V((4, seq_loc, d_model), BF16), V((n_tok, d_model), BF16), V((n_dev, d_model, 2 * HEAD_DIM), BF16),
            V((n_dev - 1,) + slab, BF16), V((n_dev,) + slab, BF16),
            V((d_model, heads_loc * HEAD_DIM), BF16), V((d_model, ff_loc), BF16), V((d_model, ff_loc), BF16),
            V((n_tok, HEAD_DIM), F32), V((n_tok, HEAD_DIM), F32),
            V((n_batch, HEAD_DIM), jnp.int32), V((seq_loc, HEAD_DIM), F32), V((seq_loc, HEAD_DIM), F32), V((n_row, HEAD_DIM), F32), V((n_row, HEAD_DIM), F32),
            V((n_batch, d_model), F32), V((n_batch, d_model), BF16), V((n_batch, d_model), BF16), V((hb, d_model), BF16),
            V((n_chip - 1, hb, d_model), BF16), V((hb, d_model), BF16), V((hb, d_model), BF16),
            V((n_row, d_model), F32), V((n_row, d_model), BF16), V((n_q, HEAD_DIM), BF16), V((2, n_q, HEAD_DIM), BF16),
            V((n_batch, HEAD_DIM), BF16), V((n_batch, HEAD_DIM), BF16),
            *state, *state, note, note,
            V(wide, F32), V(wide[1:], F32), V(wide[1:], F32), V((n_chip - 1,) + wide[2:], F32), V(wide, BF16), V(wide[2:], F32),
            V((n_row, d_model), BF16),
            V(wide, F32), V(wide[1:], F32), V(wide[1:], F32), V((n_chip - 1,) + wide[2:], F32), V(wide, BF16),
            DMA((4,)), DMA((5,)), DMA((14,)), DMA((4 * n_dev,)), DMA((5,)), DMA((n_dev,)), DMA((4 * N_BULK,)), DMA((4 * N_BULK,)), DMA((4,)), DMA((4,)),
            DMA((5,)), DMA((5,)), DMA((2 + 2 * n_dev,)), DMA((8,)), DMA((8,)), DMA((16,)), DMA((16,)),
        ]
        cache_rows = (seq_loc * n_dev + 1) * n_batch
        cache = jax.ShapeDtypeStruct((cache_rows, HEAD_DIM), BF16)
        tok = jax.ShapeDtypeStruct((n_batch, d_model), BF16)
        made = pl.pallas_call(
            functools.partial(kernel, n_dev, n_batch, seq_loc, d_model, heads_loc, ff_loc, N_BULK, PLAN),
            out_shape=[tok, tok, cache, cache],
            in_specs=[pl.BlockSpec(memory_space=pltpu.SMEM), hbm] + [vm] * 3 + [hbm] * 7,
            out_specs=[vm, vm, hbm, hbm],
            scratch_shapes=scratch,
            compiler_params=pltpu.CompilerParams(collective_id=0, has_side_effects=True, vmem_limit_bytes=67_043_328),
        )(lengths, prompt, new_tok, norm_attn, norm_mlp, w_q[0], w_k[0], w_v[0], w_o[0], w_gate[0], w_up[0], w_down[0])
        n_part = next(p for p in range(4, cache_rows) if cache_rows // n_batch % p == 0)
        last, dec, kc, vc = pl.pallas_call(
            functools.partial(write_kernel, n_part),
            out_shape=[tok, tok, cache, cache],
            in_specs=[hbm] * 4,
            out_specs=[hbm] * 4,
            scratch_shapes=[V((2, n_batch, d_model), BF16), V((2, cache_rows, HEAD_DIM), BF16), DMA((2 + 2 * n_part,)), DMA((2 + 2 * n_part,))],
        )(*made)

        def as_cache(arr):
            return jnp.transpose(arr.reshape(1, seq_loc * n_dev + 1, 1, n_batch, HEAD_DIM), (0, 3, 1, 2, 4))

        return dec, last, as_cache(kc), as_cache(vc)

    return jax.shard_map(per_device, mesh=mesh, in_specs=in_specs, out_specs=out_specs, check_vma=False)
```

time: 179 us -> 159 us (0.89)
  local copies, waits for them, and re-layouts: 10.6 us -> 0 us
  Pallas kernels: 164 us -> 157 us
  other arithmetic: 3.18 us -> 0 us
    pallas_call x1, Pallas kernels: 164 us -> 152 us  [per_device(): pl.pallas_call(functools.partial(kernel, n_dev, n_batch, seq_loc, d_model...]
    unnamed x6 -> x0, local copies, waits for them, and re-layouts: 9.15 us -> none
    pallas_call x0 -> x1, Pallas kernels: none -> 5.76 us  [per_device(): pl.pallas_call(functools.partial(write_kernel, n_part), out_shape=[tok, t...]
where the time goes in v3:
time: 159 us; the launch traced here: 158 us
  Pallas kernels  157 us (99%)
    pallas_call x1, Pallas kernels, per_device(): pl.pallas_call(functools.partial(kernel, n_dev, n_batch, seq_loc, d_model...  152 us
    pallas_call x1, Pallas kernels, per_device(): pl.pallas_call(functools.partial(write_kernel, n_part), out_shape=[tok, t...  5.76 us

profile of v3, /device:TPU:112, one launch (start us, length us, event | category | flops | bytes accessed | tf_op | source)
XLA Modules:
  0.0 158.1 jit_solution(11022120726763896364)
XLA Ops:
  0.6 151.5 %shard_map.147 = (bf16[32,3072]{1,0:T(8,128)(2,1)}, bf16[32,3072]{1,0:T(8,128)(2,1)}, bf16[12320,128]{1,0:T(8,128)(2,1)}, bf16[12320,128]{1,0:T(8,128)(2,1)}) custom-call(s32[32]{0:T(128)} %lens.1, bf16[32,48,3072]{2,1,0:T(8,128)(2,1)} %prompt.1, bf16[32,3072]{1,0:T(8,128)(2,1)} %new_tok.1, bf16[1,3072]{1,0:T(2,128)(2,1)} %g_attn.1, bf16[1,3072]{1,0:T(2,128)(2,1)} %g_mlp.1, ...), custom_call_target="tpu_custom_call" | custom-call | tf_op jit(solution)/shard_map/pallas_call | solution.py:514
  152.2 5.8 %shard_map.148 = (bf16[32,3072]{1,0:T(8,128)(2,1)}, bf16[32,3072]{1,0:T(8,128)(2,1)}, bf16[12320,128]{1,0:T(8,128)(2,1)}, bf16[12320,128]{1,0:T(8,128)(2,1)}) custom-call(bf16[32,3072]{1,0:T(8,128)(2,1)} %get-tuple-element.12.last_in, bf16[32,3072]{1,0:T(8,128)(2,1)} %get-tuple-element.13.dec_in, bf16[12320,128]{1,0:T(8,128)(2,1)} %get-tuple-element.14.k_in, ...), custom_call_target="tpu_custom_call" | custom-call | tf_op jit(solution)/shard_map/pallas_call | solution.py:523

commit v4 on v3

--- a/solution.py
+++ b/solution.py
@@ -49,11 +49,14 @@
     n_tok = n_batch * seq_loc
     n_row = 2 * n_batch
     piece = n_row // n_dev
-    half = d_model // 2
+    quarter = d_model // 4
     me = lax.axis_index('model')
     c = me // CORES
     k = me % CORES
     o_core = 1 - k
+    replica = lax.axis_index('replica')
+    odd = lax.rem(replica, 2)
+    partner = {'replica': replica + 1 - 2 * odd}
 
     def dev(rel, kk):
         chip = lax.rem(c + rel, n_chip)
@@ -65,8 +68,9 @@
         return rel * CORES + kk
 
     def rcopy(src, dst, ssem, rsem, target):
+        target = target if isinstance(target, dict) else {'model': target}
         return pltpu.make_async_remote_copy(src_ref=src, dst_ref=dst, send_sem=ssem, recv_sem=rsem,
-                                            device_id={'model': target}, device_id_type=MESH_ID)
+                                            device_id=target, device_id_type=MESH_ID)
 
     own_w = slot(0, 0)
     ld_wk = pltpu.make_async_copy(wk, wbuf.at[own_w, :, pl.ds(0, HEAD_DIM)], ldsem.at[0])
@@ -84,13 +88,17 @@
     barrier = pltpu.get_barrier_semaphore()
     for d in range(1, n_dev):
         pl.semaphore_signal(barrier, inc=1, device_id={'model': lax.rem(me + d, n_dev)}, device_id_type=MESH_ID)
-    pl.semaphore_wait(barrier, n_dev - 1)
-
-    def w_half(sl, h):
-        return wbuf.at[sl, pl.ds(h * half, half), :]
-
-    def w_copy(n, src_slot, dst_slot, h, target):
-        return rcopy(w_half(src_slot, h), w_half(dst_slot, h), w_send.at[n], w_recv.at[dst_slot * 2 + h], target)
+    pl.semaphore_signal(barrier, inc=1, device_id=partner, device_id_type=MESH_ID)
+    pl.semaphore_wait(barrier, n_dev)
+
+    order = [i + odd * (3 - 2 * i) for i in range(4)]
+
+    def w_part(sl, i):
+        return wbuf.at[sl, pl.ds(pl.multiple_of(order[i] * quarter, quarter), quarter), :]
+
+    def w_copy(n, src_slot, dst_slot, i, target, i_there=None):
+        sem = w_recv.at[dst_slot * 4 + (i if i_there is None else i_there)]
+        return rcopy(w_part(src_slot, i), w_part(dst_slot, i), w_send.at[n], sem, target)
 
     ld_wk.wait()
     ld_wv.wait()
@@ -101,19 +109,17 @@
         sends.append(cp)
         return cp
 
-    to_r = [w_copy(0, own_w, slot(LEFT, 0), 0, dev(RIGHT, 0)), w_copy(1, own_w, slot(LEFT, 0), 1, dev(RIGHT, 0))]
-    to_l = [w_copy(2, own_w, slot(RIGHT, 0), 1, dev(LEFT, 0)), w_copy(3, own_w, slot(RIGHT, 0), 0, dev(LEFT, 0))]
-    to_s = [w_copy(4, own_w, slot(0, 1), 0, dev(0, 1)), w_copy(5, own_w, slot(0, 1), 1, dev(0, 1))]
-    for cp in (to_r[0], to_l[0], to_s[0], to_s[1]):
+    to_r = [w_copy(i, own_w, slot(LEFT, 0), i, dev(RIGHT, 0)) for i in range(3)]
+    to_l = [w_copy(3 + i, own_w, slot(RIGHT, 0), i, dev(LEFT, 0)) for i in range(3)]
+    to_s = rcopy(wbuf.at[own_w], wbuf.at[slot(0, 1)], w_send.at[6], w_recv.at[slot(0, 1) * 4], dev(0, 1))
+    for cp in (to_r[0], to_l[0], to_r[1], to_l[1], to_s):
         go(cp)
-    fwd_r = w_copy(6, slot(LEFT, 0), slot(OPP, 0), 0, dev(RIGHT, 0))
-    fwd_l = w_copy(7, slot(RIGHT, 0), slot(OPP, 0), 1, dev(LEFT, 0))
-    sib_fwd = {}
-    n = 8
-    for rel in (LEFT, RIGHT, OPP):
-        for h in range(2):
-            sib_fwd[rel, h] = w_copy(n, slot(rel, 0), slot(rel, 1), h, dev(0, 1))
-            n += 1
+    fwd_r = w_copy(7, slot(LEFT, 0), slot(OPP, 0), 0, dev(RIGHT, 0))
+    fwd_l = w_copy(8, slot(RIGHT, 0), slot(OPP, 0), 1, dev(LEFT, 0))
+    to_p = {(rel, i): w_copy(9 + n, slot(rel, 0), slot(rel, 0), i, partner, 3 - i)
+            for n, (rel, i) in enumerate(((LEFT, 0), (RIGHT, 0), (OPP, 0), (OPP, 1)))}
+    sib_fwd = {(rel, i): w_copy(13 + 4 * n + i, slot(rel, 0), slot(rel, 1), i, dev(0, 1))
+               for n, rel in enumerate((LEFT, RIGHT, OPP)) for i in range(4)}
 
     ld_wq = pltpu.make_async_copy(wq, wq_v, ldsem.at[2])
     ld_wg = pltpu.make_async_copy(wg, wg_v, ldsem.at[3])
@@ -162,8 +168,8 @@
     oth_rows = pl.ds(pl.multiple_of(o_core * hb, hb), hb)
     xl_sum[...] = xl_own[my_rows, :] + xl_sib[my_rows, :]
     xl_b = [go(rcopy(xl_sum, xl_recv.at[n_chip - 1 - rel], xl_send.at[rel], xl_rsem.at[n_chip - rel], dev(rel, 0))) for rel in (RIGHT, LEFT, OPP)]
-    go(to_r[1])
-    go(to_l[1])
+    go(to_r[2])
+    go(to_l[2])
 
     def head(sl, dst):
         for_rows = 512
@@ -186,21 +192,25 @@
         sl = slot((n_chip - rel) % n_chip, kk)
         return rcopy(stage.at[slot(rel, kk) - 1], kvrecv.at[sl], kv_send.at[n], kv_recv.at[sl], dev(rel, kk))
 
-    def wait_w(rel, kk, h):
-        w_copy(0, slot(rel, kk), slot(rel, kk), h, dev(0, 1)).wait_recv()
-
+    def wait_w(rel, kk, i):
+        w_copy(0, slot(rel, kk), slot(rel, kk), i, dev(0, 1)).wait_recv()
+
+    for rel in (LEFT, RIGHT):
+        wait_w(rel, 0, 0)
+        go(to_p[rel, 0])
+        go(sib_fwd[rel, 0])
+        if rel == LEFT:
+            go(fwd_r)
     head(own_w, kvrecv.at[own_w])
-    wait_w(0, 1, 0)
-    wait_w(0, 1, 1)
+    for rel in (RIGHT, LEFT):
+        wait_w(rel, 0, 1)
+        if rel == RIGHT:
+            go(fwd_l)
+        go(sib_fwd[rel, 1])
+    to_s.wait_recv()
     head(slot(0, 1), stage.at[slot(0, 1) - 1])
     kv_sib = go(kv_copy(0, 0, 1))
 
-    wait_w(LEFT, 0, 0)
-    go(fwd_r)
-    go(sib_fwd[LEFT, 0])
-    wait_w(RIGHT, 0, 1)
-    go(fwd_l)
-    go(sib_fwd[RIGHT, 1])
     for cp in xl_b:
         cp.wait_recv()
     xl_half[...] = xl_sum[...] + xl_recv[0] + (xl_recv[1] + xl_recv[2])
@@ -228,24 +238,25 @@
     for cp in outs:
         cp.start()
 
-    wait_w(LEFT, 0, 1)
-    go(sib_fwd[LEFT, 1])
-    wait_w(RIGHT, 0, 0)
-    go(sib_fwd[RIGHT, 0])
+    for rel in (LEFT, RIGHT):
+        for i in (3, 2):
+            wait_w(rel, 0, i)
+            go(sib_fwd[rel, i])
     n = 1
     kv_nb = {}
     for kk in range(2):
         for rel in (RIGHT, LEFT):
             if kk == 1:
-                wait_w(rel, 1, 0)
-                wait_w(rel, 1, 1)
+                for i in range(4):
+                    wait_w(rel, 1, i)
             head(slot(rel, kk), stage.at[slot(rel, kk) - 1])
             kv_nb[rel, kk] = go(kv_copy(n, rel, kk))
             n += 1
-    wait_w(OPP, 0, 0)
-    go(sib_fwd[OPP, 0])
-    wait_w(OPP, 0, 1)
-    go(sib_fwd[OPP, 1])
+        if kk == 0:
+            for i in range(2):
+                wait_w(OPP, 0, i)
+                go(to_p[OPP, i])
+                go(sib_fwd[OPP, i])
 
     scale = HEAD_DIM ** -0.5
     n_q = heads_loc * n_row
@@ -293,12 +304,33 @@
         cols = [jnp.sum(jnp.where(on_diag(size), ref[pl.ds(r0 + j, 1), :], 0.0), axis=1, keepdims=True) for j, (i, size) in enumerate(lane_rows)]
         return jnp.concatenate(cols, axis=0)
 
+    def put_out(n, sl, src):
+        rows = pl.ds(pl.multiple_of(src * n_tok, n_tok), n_tok)
+        for i, ref in enumerate((kout, vout)):
+            cp = pltpu.make_async_copy(kvrecv.at[sl, i], ref.at[rows, :], out_sem.at[2 + 2 * n + i])
+            cp.start()
+            outs.append(cp)
+
+    reset(mine)
+    col = lax.broadcasted_iota(jnp.int32, (n_q, n_batch), 1)
+    row = lax.broadcasted_iota(jnp.int32, (n_q, n_batch), 0)
+    is_new = (row // n_batch) % 2 == 1
+    update(mine, dot_bt(q_s[...], knew[...]), (col == row % n_batch) & is_new, vnew[...])
+    put_out(0, own_w, me)
+    attend(mine, q_s, kvrecv.at[own_w], me)
+    kv_sib.wait_recv()
+    put_out(1, slot(0, 1), dev(0, 1))
+    attend(mine, q_s, kvrecv.at[slot(0, 1)], dev(0, 1))
+
     n_lr = len(lane_rows)
     pt_out = []
+    for i in (3, 2):
+        wait_w(OPP, 0, i)
+        go(sib_fwd[OPP, i])
     for kk in range(2):
         if kk == 1:
-            wait_w(OPP, 1, 0)
-            wait_w(OPP, 1, 1)
+            for i in range(4):
+                wait_w(OPP, 1, i)
         block = stage.at[slot(OPP, kk) - 1]
         head(slot(OPP, kk), block)
         q_out[kk].wait_recv()
@@ -334,23 +366,6 @@
     ld_wo.start()
     ld_wd.start()
 
-    def put_out(n, sl, src):
-        rows = pl.ds(pl.multiple_of(src * n_tok, n_tok), n_tok)
-        for i, ref in enumerate((kout, vout)):
-            cp = pltpu.make_async_copy(kvrecv.at[sl, i], ref.at[rows, :], out_sem.at[2 + 2 * n + i])
-            cp.start()
-            outs.append(cp)
-
-    reset(mine)
-    col = lax.broadcasted_iota(jnp.int32, (n_q, n_batch), 1)
-    row = lax.broadcasted_iota(jnp.int32, (n_q, n_batch), 0)
-    is_new = (row // n_batch) % 2 == 1
-    update(mine, dot_bt(q_s[...], knew[...]), (col == row % n_batch) & is_new, vnew[...])
-    put_out(0, own_w, me)
-    attend(mine, q_s, kvrecv.at[own_w], me)
-    kv_sib.wait_recv()
-    put_out(1, slot(0, 1), dev(0, 1))
-    attend(mine, q_s, kvrecv.at[slot(0, 1)], dev(0, 1))
     n = 2
     for kk in range(2):
         for rel in (RIGHT, LEFT):
@@ -461,7 +476,7 @@
 
 def solution(mesh):
     n_dev = mesh.shape['model']
-    assert n_dev == 4 * CORES
+    assert n_dev == 4 * CORES and mesh.shape['replica'] % 2 == 0
     seq_spec = P('replica', 'model', None)
     col_spec = P(None, None, 'model')
     row_spec = P(None, 'model', None)
@@ -505,7 +520,7 @@
             V(wide, F32), V(wide[1:], F32), V(wide[1:], F32), V((n_chip - 1,) + wide[2:], F32), V(wide, BF16), V(wide[2:], F32),
             V((n_row, d_model), BF16),
             V(wide, F32), V(wide[1:], F32), V(wide[1:], F32), V((n_chip - 1,) + wide[2:], F32), V(wide, BF16),
-            DMA((4,)), DMA((5,)), DMA((14,)), DMA((4 * n_dev,)), DMA((5,)), DMA((n_dev,)), DMA((4 * N_BULK,)), DMA((4 * N_BULK,)), DMA((4,)), DMA((4,)),
+            DMA((4,)), DMA((5,)), DMA((25,)), DMA((4 * n_dev,)), DMA((5,)), DMA((n_dev,)), DMA((4 * N_BULK,)), DMA((4 * N_BULK,)), DMA((4,)), DMA((4,)),
             DMA((5,)), DMA((5,)), DMA((2 + 2 * n_dev,)), DMA((8,)), DMA((8,)), DMA((16,)), DMA((16,)),
         ]
         cache_rows = (seq_loc * n_dev + 1) * n_batch

time: 159 us -> 143 us (0.90)
  Pallas kernels: 157 us -> 141 us
    pallas_call x1, Pallas kernels: 152 us -> 135 us  [per_device(): pl.pallas_call(functools.partial(kernel, n_dev, n_batch, seq_loc, d_model...]
where the time goes in v4:
time: 143 us; the launch traced here: 141 us
  Pallas kernels  141 us (99%)
    pallas_call x1, Pallas kernels, per_device(): pl.pallas_call(functools.partial(kernel, n_dev, n_batch, seq_loc, d_model...  135 us
    pallas_call x1, Pallas kernels, per_device(): pl.pallas_call(functools.partial(write_kernel, n_part), out_shape=[tok, t...  5.76 us

profile of v4, /device:TPU:112, one launch (start us, length us, event | category | flops | bytes accessed | tf_op | source)
XLA Modules:
  0.0 141.3 jit_solution(9275551398194300824)
XLA Ops:
  0.6 134.8 %shard_map.147 = (bf16[32,3072]{1,0:T(8,128)(2,1)}, bf16[32,3072]{1,0:T(8,128)(2,1)}, bf16[12320,128]{1,0:T(8,128)(2,1)}, bf16[12320,128]{1,0:T(8,128)(2,1)}) custom-call(s32[32]{0:T(128)} %lens.1, bf16[32,48,3072]{2,1,0:T(8,128)(2,1)} %prompt.1, bf16[32,3072]{1,0:T(8,128)(2,1)} %new_tok.1, bf16[1,3072]{1,0:T(2,128)(2,1)} %g_attn.1, bf16[1,3072]{1,0:T(2,128)(2,1)} %g_mlp.1, ...), custom_call_target="tpu_custom_call" | custom-call | tf_op jit(solution)/shard_map/pallas_call | solution.py:529
  135.4 5.8 %shard_map.148 = (bf16[32,3072]{1,0:T(8,128)(2,1)}, bf16[32,3072]{1,0:T(8,128)(2,1)}, bf16[12320,128]{1,0:T(8,128)(2,1)}, bf16[12320,128]{1,0:T(8,128)(2,1)}) custom-call(bf16[32,3072]{1,0:T(8,128)(2,1)} %get-tuple-element.12.last_in, bf16[32,3072]{1,0:T(8,128)(2,1)} %get-tuple-element.13.dec_in, bf16[12320,128]{1,0:T(8,128)(2,1)} %get-tuple-element.14.k_in, ...), custom_call_target="tpu_custom_call" | custom-call | tf_op jit(solution)/shard_map/pallas_call | solution.py:538

commit v5 on v4

--- a/solution.py
+++ b/solution.py
@@ -37,13 +37,13 @@
 
 def kernel(n_dev, n_batch, seq_loc, d_model, heads_loc, ff_loc, n_bulk, plan,
            lens, prompt, new_tok, g_attn, g_mlp, wq, wk, wv, wo, wg, wu, wd,
-           last_out, dec_out, kout, vout,
-           xbuf, normed, wbuf, stage, kvrecv, wq_v, wg_v, wu_v, res_k, res_v,
+           last_out, dec_out, kvrecv, kvnew,
+           xbuf, normed, wbuf, stage, wq_v, wg_v, wu_v, res_k, res_v,
            len_v, cos_pos, sin_pos, cos_row, sin_row,
-           last_f, xl_own, xl_sib, xl_sum, xl_recv, xl_half, xl_oth, rows_f, rows_n, q_s, q_in, knew, vnew,
+           last_f, xl_own, xl_sib, xl_sum, xl_recv, xl_half, xl_oth, rows_f, rows_n, q_s, q_in,
            m_s, l_s, acc_s, m_p, l_p, acc_p, msg, msg_in,
            part, d2d_in, rs_sum, rs_in, agbuf, x1_f, hid_n, part2, d2d_in2, rs_sum2, rs_in2, agbuf2,
-           xsem, ldsem, w_send, w_recv, kv_send, kv_recv, bulk_send, bulk_recv, pt_send, pt_recv, xl_send, xl_rsem, out_sem,
+           xsem, ldsem, w_send, w_recv, kv_send, kv_recv, bulk_send, bulk_recv, pt_send, pt_recv, xl_send, xl_rsem,
            ar_send, ar_recv, ag_send, ag_recv):
     n_chip = n_dev // CORES
     n_tok = n_batch * seq_loc
@@ -230,13 +230,8 @@
     kv_new = dot_f32(rows_n[...], wbuf[own_w])
     new_rows = slice(n_batch, n_row)
     k_new = rotate(kv_new[new_rows, :HEAD_DIM], cos_row[pl.ds(n_batch, n_batch), :], sin_row[pl.ds(n_batch, n_batch), :])
-    knew[...] = k_new.astype(BF16)
-    vnew[...] = kv_new[new_rows, HEAD_DIM:].astype(BF16)
-    tail_row = n_dev * n_tok
-    outs = [pltpu.make_async_copy(knew, kout.at[pl.ds(tail_row, n_batch), :], out_sem.at[0]),
-            pltpu.make_async_copy(vnew, vout.at[pl.ds(tail_row, n_batch), :], out_sem.at[1])]
-    for cp in outs:
-        cp.start()
+    kvnew[0] = k_new.astype(BF16)
+    kvnew[1] = kv_new[new_rows, HEAD_DIM:].astype(BF16)
 
     for rel in (LEFT, RIGHT):
         for i in (3, 2):
@@ -304,22 +299,13 @@
         cols = [jnp.sum(jnp.where(on_diag(size), ref[pl.ds(r0 + j, 1), :], 0.0), axis=1, keepdims=True) for j, (i, size) in enumerate(lane_rows)]
         return jnp.concatenate(cols, axis=0)
 
-    def put_out(n, sl, src):
-        rows = pl.ds(pl.multiple_of(src * n_tok, n_tok), n_tok)
-        for i, ref in enumerate((kout, vout)):
-            cp = pltpu.make_async_copy(kvrecv.at[sl, i], ref.at[rows, :], out_sem.at[2 + 2 * n + i])
-            cp.start()
-            outs.append(cp)
-
     reset(mine)
     col = lax.broadcasted_iota(jnp.int32, (n_q, n_batch), 1)
     row = lax.broadcasted_iota(jnp.int32, (n_q, n_batch), 0)
     is_new = (row // n_batch) % 2 == 1
-    update(mine, dot_bt(q_s[...], knew[...]), (col == row % n_batch) & is_new, vnew[...])
-    put_out(0, own_w, me)
+    update(mine, dot_bt(q_s[...], kvnew[0]), (col == row % n_batch) & is_new, kvnew[1])
     attend(mine, q_s, kvrecv.at[own_w], me)
     kv_sib.wait_recv()
-    put_out(1, slot(0, 1), dev(0, 1))
     attend(mine, q_s, kvrecv.at[slot(0, 1)], dev(0, 1))
 
     n_lr = len(lane_rows)
@@ -371,7 +357,6 @@
         for rel in (RIGHT, LEFT):
             src_rel = (n_chip - rel) % n_chip
             kv_nb[rel, kk].wait_recv()
-            put_out(n, slot(src_rel, kk), dev(src_rel, kk))
             attend(mine, q_s, kvrecv.at[slot(src_rel, kk)], dev(src_rel, kk))
             n += 1
     for kk in range(2):
@@ -448,29 +433,27 @@
     for kk in range(2):
         for cp in bulk[kk * 2 * n_bulk:(kk + 1) * 2 * n_bulk]:
             cp.wait_recv()
-        put_out(n, slot(OPP, kk), dev(OPP, kk))
         n += 1
     for cp in sends:
         cp.wait_send()
-    for cp in outs:
-        cp.wait()
-
-
-def write_kernel(n_part, last_in, dec_in, k_in, v_in, last_out, dec_out, k_out, v_out, tok_v, kv_v, in_sem, out_sem):
-    rows = k_in.shape[0] // n_part
-    pairs = [(last_in, last_out, tok_v.at[0]), (dec_in, dec_out, tok_v.at[1])]
-    for p in range(n_part):
-        for i, (src, dst) in enumerate(((k_in, k_out), (v_in, v_out))):
-            r = pl.ds(p * rows, rows)
-            pairs.append((src.at[r, :], dst.at[r, :], kv_v.at[i, r, :]))
-    loads = [pltpu.make_async_copy(src, buf, in_sem.at[n]) for n, (src, dst, buf) in enumerate(pairs)]
-    stores = [pltpu.make_async_copy(buf, dst, out_sem.at[n]) for n, (src, dst, buf) in enumerate(pairs)]
-    for cp in loads:
+
+
+def write_kernel(n_dev, last_in, dec_in, kv, kv_new, last_out, dec_out, k_out, v_out, sem):
+    n_tok = kv.shape[2]
+    n_batch = kv_new.shape[1]
+    me = lax.axis_index('model')
+    pairs = [(last_in, last_out), (dec_in, dec_out)]
+    for i, ref in enumerate((k_out, v_out)):
+        pairs.append((kv_new.at[i], ref.at[pl.ds(n_dev * n_tok, n_batch), :]))
+        for sl in range(n_dev):
+            chip = lax.rem(me // CORES + sl // CORES, n_dev // CORES)
+            core = lax.rem(me + sl, CORES)
+            src = pl.ds(pl.multiple_of((CORES * chip + core) * n_tok, n_tok), n_tok)
+            pairs.append((kv.at[sl, i], ref.at[src, :]))
+    copies = [pltpu.make_async_copy(src, dst, sem.at[n]) for n, (src, dst) in enumerate(pairs)]
+    for cp in copies:
         cp.start()
-    for ld, st in zip(loads, stores):
-        ld.wait()
-        st.start()
-    for cp in stores:
+    for cp in copies:
         cp.wait()
 
 
@@ -508,39 +491,38 @@
         note = V((2, pl.cdiv(n_q + n_lr, 8) * 8, HEAD_DIM), F32)
         scratch = [
             V((4, seq_loc, d_model), BF16), V((n_tok, d_model), BF16), V((n_dev, d_model, 2 * HEAD_DIM), BF16),
-            V((n_dev - 1,) + slab, BF16), V((n_dev,) + slab, BF16),
+            V((n_dev - 1,) + slab, BF16),
             V((d_model, heads_loc * HEAD_DIM), BF16), V((d_model, ff_loc), BF16), V((d_model, ff_loc), BF16),
             V((n_tok, HEAD_DIM), F32), V((n_tok, HEAD_DIM), F32),
             V((n_batch, HEAD_DIM), jnp.int32), V((seq_loc, HEAD_DIM), F32), V((seq_loc, HEAD_DIM), F32), V((n_row, HEAD_DIM), F32), V((n_row, HEAD_DIM), F32),
             V((n_batch, d_model), F32), V((n_batch, d_model), BF16), V((n_batch, d_model), BF16), V((hb, d_model), BF16),
             V((n_chip - 1, hb, d_model), BF16), V((hb, d_model), BF16), V((hb, d_model), BF16),
             V((n_row, d_model), F32), V((n_row, d_model), BF16), V((n_q, HEAD_DIM), BF16), V((2, n_q, HEAD_DIM), BF16),
-            V((n_batch, HEAD_DIM), BF16), V((n_batch, HEAD_DIM), BF16),
             *state, *state, note, note,
             V(wide, F32), V(wide[1:], F32), V(wide[1:], F32), V((n_chip - 1,) + wide[2:], F32), V(wide, BF16), V(wide[2:], F32),
             V((n_row, d_model), BF16),
             V(wide, F32), V(wide[1:], F32), V(wide[1:], F32), V((n_chip - 1,) + wide[2:], F32), V(wide, BF16),
             DMA((4,)), DMA((5,)), DMA((25,)), DMA((4 * n_dev,)), DMA((5,)), DMA((n_dev,)), DMA((4 * N_BULK,)), DMA((4 * N_BULK,)), DMA((4,)), DMA((4,)),
-            DMA((5,)), DMA((5,)), DMA((2 + 2 * n_dev,)), DMA((8,)), DMA((8,)), DMA((16,)), DMA((16,)),
+            DMA((5,)), DMA((5,)), DMA((8,)), DMA((8,)), DMA((16,)), DMA((16,)),
         ]
         cache_rows = (seq_loc * n_dev + 1) * n_batch
         cache = jax.ShapeDtypeStruct((cache_rows, HEAD_DIM), BF16)
         tok = jax.ShapeDtypeStruct((n_batch, d_model), BF16)
         made = pl.pallas_call(
             functools.partial(kernel, n_dev, n_batch, seq_loc, d_model, heads_loc, ff_loc, N_BULK, PLAN),
+            out_shape=[V((n_batch, d_model), BF16), V((n_batch, d_model), BF16), V((n_dev,) + slab, BF16), V((2, n_batch, HEAD_DIM), BF16)],
+            in_specs=[pl.BlockSpec(memory_space=pltpu.SMEM), hbm] + [vm] * 3 + [hbm] * 7,
+            out_specs=[vm] * 4,
+            scratch_shapes=scratch,
+            compiler_params=pltpu.CompilerParams(collective_id=0, has_side_effects=True, vmem_limit_bytes=60_300_000),
+        )(lengths, prompt, new_tok, norm_attn, norm_mlp, w_q[0], w_k[0], w_v[0], w_o[0], w_gate[0], w_up[0], w_down[0])
+        last, dec, kc, vc = pl.pallas_call(
+            functools.partial(write_kernel, n_dev),
             out_shape=[tok, tok, cache, cache],
-            in_specs=[pl.BlockSpec(memory_space=pltpu.SMEM), hbm] + [vm] * 3 + [hbm] * 7,
-            out_specs=[vm, vm, hbm, hbm],
-            scratch_shapes=scratch,
-            compiler_params=pltpu.CompilerParams(collective_id=0, has_side_effects=True, vmem_limit_bytes=67_043_328),
-        )(lengths, prompt, new_tok, norm_attn, norm_mlp, w_q[0], w_k[0], w_v[0], w_o[0], w_gate[0], w_up[0], w_down[0])
-        n_part = next(p for p in range(4, cache_rows) if cache_rows // n_batch % p == 0)
-        last, dec, kc, vc = pl.pallas_call(
-            functools.partial(write_kernel, n_part),
-            out_shape=[tok, tok, cache, cache],
-            in_specs=[hbm] * 4,
+            in_specs=[vm] * 4,
             out_specs=[hbm] * 4,
-            scratch_shapes=[V((2, n_batch, d_model), BF16), V((2, cache_rows, HEAD_DIM), BF16), DMA((2 + 2 * n_part,)), DMA((2 + 2 * n_part,))],
+            scratch_shapes=[DMA((4 + 2 * n_dev,))],
+            compiler_params=pltpu.CompilerParams(vmem_limit_bytes=1 << 20),
         )(*made)
 
         def as_cache(arr):

time: 143 us -> 138 us (0.965)
  Pallas kernels: 141 us -> 136 us
    pallas_call x1, Pallas kernels: 5.76 us -> 2.94 us  [per_device(): pl.pallas_call(functools.partial(write_kernel, n_dev), out_shape=[tok, to...]
    pallas_call x1, Pallas kernels: 135 us -> 133 us  [per_device(): pl.pallas_call(functools.partial(kernel, n_dev, n_batch, seq_loc, d_model...]
where the time goes in v5:
time: 138 us; the launch traced here: 137 us
  Pallas kernels  136 us (99%)
    pallas_call x1, Pallas kernels, per_device(): pl.pallas_call(functools.partial(kernel, n_dev, n_batch, seq_loc, d_model...  133 us
    pallas_call x1, Pallas kernels, per_device(): pl.pallas_call(functools.partial(write_kernel, n_dev), out_shape=[tok, to...  2.94 us

profile of v5, /device:TPU:112, one launch (start us, length us, event | category | flops | bytes accessed | tf_op | source)
XLA Modules:
  0.0 136.8 jit_solution(11895636122826156424)
XLA Ops:
  0.6 133.1 %shard_map.147 = (bf16[32,3072]{1,0:T(8,128)(2,1)S(1)}, bf16[32,3072]{1,0:T(8,128)(2,1)S(1)}, bf16[8,2,1536,128]{3,2,1,0:T(8,128)(2,1)S(1)}, bf16[2,32,128]{2,1,0:T(8,128)(2,1)S(1)}) custom-call(s32[32]{0:T(128)} %lens.1, bf16[32,48,3072]{2,1,0:T(8,128)(2,1)} %prompt.1, bf16[32,3072]{1,0:T(8,128)(2,1)} %new_tok.1, bf16[1,3072]{1,0:T(2,128)(2,1)} %g_attn.1, ...), custom_call_target="tpu_custom_call" | custom-call | tf_op jit(solution)/shard_map/pallas_call | solution.py:511
  133.7 2.9 %shard_map.148 = (bf16[32,3072]{1,0:T(8,128)(2,1)}, bf16[32,3072]{1,0:T(8,128)(2,1)}, bf16[12320,128]{1,0:T(8,128)(2,1)}, bf16[12320,128]{1,0:T(8,128)(2,1)}) custom-call(bf16[32,3072]{1,0:T(8,128)(2,1)S(1)} %get-tuple-element.12.last_in, bf16[32,3072]{1,0:T(8,128)(2,1)S(1)} %get-tuple-element.13.dec_in, bf16[8,2,1536,128]{3,2,1,0:T(8,128)(2,1)S(1)} %get-tuple-element.14.kv, ...), custom_call_target="tpu_custom_call" | custom-call | tf_op jit(solution)/shard_map/pallas_call | solution.py:519

commit v6 on v5

--- a/solution.py
+++ b/solution.py
@@ -226,7 +226,8 @@
     for g in range(heads_loc):
         q_g = rotate(q_all[:, g * HEAD_DIM:(g + 1) * HEAD_DIM], cos_row[...], sin_row[...])
         q_s[pl.ds(g * n_row, n_row), :] = q_g.astype(BF16)
-    q_out = [go(rcopy(q_s, q_in.at[kk], pt_send.at[kk], pt_recv.at[kk], dev(OPP, kk))) for kk in range(2)]
+    q_out = go(rcopy(q_s, q_in.at[0], pt_send.at[0], pt_recv.at[0], dev(OPP, 0)))
+    q_fwd = rcopy(q_in.at[0], q_in.at[1], pt_send.at[1], pt_recv.at[1], dev(0, 1))
     kv_new = dot_f32(rows_n[...], wbuf[own_w])
     new_rows = slice(n_batch, n_row)
     k_new = rotate(kv_new[new_rows, :HEAD_DIM], cos_row[pl.ds(n_batch, n_batch), :], sin_row[pl.ds(n_batch, n_batch), :])
@@ -252,6 +253,8 @@
                 wait_w(OPP, 0, i)
                 go(to_p[OPP, i])
                 go(sib_fwd[OPP, i])
+    q_out.wait_recv()
+    go(q_fwd)
 
     scale = HEAD_DIM ** -0.5
     n_q = heads_loc * n_row
@@ -309,24 +312,41 @@
     attend(mine, q_s, kvrecv.at[slot(0, 1)], dev(0, 1))
 
     n_lr = len(lane_rows)
-    pt_out = []
+    other = (m_p, l_p, acc_p)
+
+    def pack(state, ref):
+        ref[pl.ds(0, n_q), :] = state[2][...]
+        put_column(ref, n_q, state[0][...])
+        put_column(ref, n_q + n_lr, state[1][...])
+
+    def merge(state, ref):
+        m_r, l_r, acc_r = state
+        m_o, l_o = get_column(ref, n_q), get_column(ref, n_q + n_lr)
+        m_old = m_r[...]
+        m_new = jnp.maximum(m_old, m_o)
+        f_mine, f_oth = jnp.exp(m_old - m_new), jnp.exp(m_o - m_new)
+        l_r[...] = l_r[...] * f_mine + l_o * f_oth
+        acc_r[...] = acc_r[...] * f_mine + ref[pl.ds(0, n_q), :] * f_oth
+        m_r[...] = m_new
+
     for i in (3, 2):
         wait_w(OPP, 0, i)
         go(sib_fwd[OPP, i])
-    for kk in range(2):
-        if kk == 1:
-            for i in range(4):
-                wait_w(OPP, 1, i)
-        block = stage.at[slot(OPP, kk) - 1]
-        head(slot(OPP, kk), block)
-        q_out[kk].wait_recv()
-        other = (m_p, l_p, acc_p)
-        reset(other)
-        attend(other, q_in.at[kk], block, me)
-        msg[kk, pl.ds(0, n_q), :] = acc_p[...]
-        put_column(msg.at[kk], n_q, m_p[...])
-        put_column(msg.at[kk], n_q + n_lr, l_p[...])
-        pt_out.append(go(rcopy(msg.at[kk], msg_in.at[kk], pt_send.at[2 + kk], pt_recv.at[2 + kk], dev(OPP, kk))))
+    for i in range(4):
+        wait_w(OPP, 1, i)
+    head(slot(OPP, 1), stage.at[slot(OPP, 1) - 1])
+    q_fwd.wait_recv()
+    reset(other)
+    attend(other, q_in.at[1], stage.at[slot(OPP, 1) - 1], me)
+    pack(other, msg.at[1])
+    pt_sib = go(rcopy(msg.at[1], msg_in.at[1], pt_send.at[2], pt_recv.at[2], dev(0, 1)))
+    head(slot(OPP, 0), stage.at[slot(OPP, 0) - 1])
+    reset(other)
+    attend(other, q_in.at[0], stage.at[slot(OPP, 0) - 1], me)
+    pt_sib.wait_recv()
+    merge(other, msg_in.at[1])
+    pack(other, msg.at[0])
+    pt_out = go(rcopy(msg.at[0], msg_in.at[0], pt_send.at[3], pt_recv.at[3], dev(OPP, 0)))
 
     per = n_tok // n_bulk
     bulk = []
@@ -359,16 +379,8 @@
             kv_nb[rel, kk].wait_recv()
             attend(mine, q_s, kvrecv.at[slot(src_rel, kk)], dev(src_rel, kk))
             n += 1
-    for kk in range(2):
-        pt_out[kk].wait_recv()
-        m_o = get_column(msg_in.at[kk], n_q)
-        l_o = get_column(msg_in.at[kk], n_q + n_lr)
-        m_old = m_s[...]
-        m_new = jnp.maximum(m_old, m_o)
-        f_mine, f_oth = jnp.exp(m_old - m_new), jnp.exp(m_o - m_new)
-        l_s[...] = l_s[...] * f_mine + l_o * f_oth
-        acc_s[...] = acc_s[...] * f_mine + msg_in[kk, pl.ds(0, n_q), :] * f_oth
-        m_s[...] = m_new
+    pt_out.wait_recv()
+    merge(mine, msg_in.at[0])
     o_all = (acc_s[...] / l_s[...]).astype(BF16)
 
     def sum_over_model(i, part_r, d2d_r, sum_r, in_r):

time: 138 us -> 135 us (0.978)
  Pallas kernels: 136 us -> 134 us
    pallas_call x1, Pallas kernels: 133 us -> 131 us  [per_device(): pl.pallas_call(functools.partial(kernel, n_dev, n_batch, seq_loc, d_model...]
where the time goes in v6:
time: 135 us
  Pallas kernels  134 us (99%)
    pallas_call x1, Pallas kernels, per_device(): pl.pallas_call(functools.partial(kernel, n_dev, n_batch, seq_loc, d_model...  131 us
    pallas_call x1, Pallas kernels, per_device(): pl.pallas_call(functools.partial(write_kernel, n_dev), out_shape=[tok, to...  2.94 us

profile of v6, /device:TPU:112, one launch (start us, length us, event | category | flops | bytes accessed | tf_op | source)
XLA Modules:
  0.0 134.5 jit_solution(17724290334583486129)
XLA Ops:
  0.6 130.8 %shard_map.147 = (bf16[32,3072]{1,0:T(8,128)(2,1)S(1)}, bf16[32,3072]{1,0:T(8,128)(2,1)S(1)}, bf16[8,2,1536,128]{3,2,1,0:T(8,128)(2,1)S(1)}, bf16[2,32,128]{2,1,0:T(8,128)(2,1)S(1)}) custom-call(s32[32]{0:T(128)} %lens.1, bf16[32,48,3072]{2,1,0:T(8,128)(2,1)} %prompt.1, bf16[32,3072]{1,0:T(8,128)(2,1)} %new_tok.1, bf16[1,3072]{1,0:T(2,128)(2,1)} %g_attn.1, ...), custom_call_target="tpu_custom_call" | custom-call | tf_op jit(solution)/shard_map/pallas_call | solution.py:523
  131.4 2.9 %shard_map.148 = (bf16[32,3072]{1,0:T(8,128)(2,1)}, bf16[32,3072]{1,0:T(8,128)(2,1)}, bf16[12320,128]{1,0:T(8,128)(2,1)}, bf16[12320,128]{1,0:T(8,128)(2,1)}) custom-call(bf16[32,3072]{1,0:T(8,128)(2,1)S(1)} %get-tuple-element.12.last_in, bf16[32,3072]{1,0:T(8,128)(2,1)S(1)} %get-tuple-element.13.dec_in, bf16[8,2,1536,128]{3,2,1,0:T(8,128)(2,1)S(1)} %get-tuple-element.14.kv, ...), custom_call_target="tpu_custom_call" | custom-call | tf_op jit(solution)/shard_map/pallas_call | solution.py:531

commit v7 on v6

--- a/solution.py
+++ b/solution.py
@@ -11,8 +11,8 @@
 HEAD_DIM = 128
 NEG_BIG = -1e30
 CORES = 2
-N_BULK = 2
-PLAN = (2, 1, 3, 1, 1)
+N_BULK = 3
+PLAN = (3, 2, 4, 2, 1)
 MESH_ID = pl.DeviceIdType.MESH
 BF16 = jnp.bfloat16
 F32 = jnp.float32

time: 135 us -> 135 us (level)
  no operation moved by 1% of the time
where the time goes in v7:
time: 135 us
  Pallas kernels  134 us (99%)
    pallas_call x1, Pallas kernels, per_device(): pl.pallas_call(functools.partial(kernel, n_dev, n_batch, seq_loc, d_model...  131 us
    pallas_call x1, Pallas kernels, per_device(): pl.pallas_call(functools.partial(write_kernel, n_dev), out_shape=[tok, to...  2.94 us

profile of v7, /device:TPU:112, one launch (start us, length us, event | category | flops | bytes accessed | tf_op | source)
XLA Modules:
  0.0 134.6 jit_solution(5736234666981435294)
XLA Ops:
  0.6 130.9 %shard_map.147 = (bf16[32,3072]{1,0:T(8,128)(2,1)S(1)}, bf16[32,3072]{1,0:T(8,128)(2,1)S(1)}, bf16[8,2,1536,128]{3,2,1,0:T(8,128)(2,1)S(1)}, bf16[2,32,128]{2,1,0:T(8,128)(2,1)S(1)}) custom-call(s32[32]{0:T(128)} %lens.1, bf16[32,48,3072]{2,1,0:T(8,128)(2,1)} %prompt.1, bf16[32,3072]{1,0:T(8,128)(2,1)} %new_tok.1, bf16[1,3072]{1,0:T(2,128)(2,1)} %g_attn.1, ...), custom_call_target="tpu_custom_call" | custom-call | tf_op jit(solution)/shard_map/pallas_call | solution.py:523
  131.5 2.9 %shard_map.148 = (bf16[32,3072]{1,0:T(8,128)(2,1)}, bf16[32,3072]{1,0:T(8,128)(2,1)}, bf16[12320,128]{1,0:T(8,128)(2,1)}, bf16[12320,128]{1,0:T(8,128)(2,1)}) custom-call(bf16[32,3072]{1,0:T(8,128)(2,1)S(1)} %get-tuple-element.12.last_in, bf16[32,3072]{1,0:T(8,128)(2,1)S(1)} %get-tuple-element.13.dec_in, bf16[8,2,1536,128]{3,2,1,0:T(8,128)(2,1)S(1)} %get-tuple-element.14.kv, ...), custom_call_target="tpu_custom_call" | custom-call | tf_op jit(solution)/shard_map/pallas_call | solution.py:531
